TPU v7x, 8 devices: a whole 2x2x1 slice. The times are simulated.
8 devices in a mesh: inst: 1 (over z), dev: 2 (over y), side: 4 (over x, core).
Axes of the slice: x: 2, y: 2, z: 1, core: 2. Of those that a mesh axis runs over, the one named last changes fastest.
Arguments:
- hidden: bfloat16 [512, 2048], P(('inst', 'dev'))
- k_cache: bfloat16 [1, 512, 16, 128, 128], P(None, ('inst', 'dev'))
- v_cache: bfloat16 [1, 512, 16, 128, 128], P(None, ('inst', 'dev'))
- cache_lens: int32 [512], P(('inst', 'dev'))
- expert_ids: int32 [1, 512, 8], P(None, ('inst', 'dev'))
- route_gates: float32 [1, 512, 8], P(None, ('inst', 'dev'))
- attn_gain: float32 [1, 2048], replicated
- ffn_gain: float32 [1, 2048], replicated
- w_q: bfloat16 [1, 2048, 2048], replicated
- w_kv: bfloat16 [1, 2048, 4096], replicated
- w_o: bfloat16 [1, 2048, 2048], replicated
- shared_gate: bfloat16 [1, 2048, 1024], replicated
- shared_up: bfloat16 [1, 2048, 1024], replicated
- shared_down: bfloat16 [1, 1024, 2048], replicated
- w_gate: bfloat16 [1, 64, 2048, 1024], P(None, 'dev')
- w_up: bfloat16 [1, 64, 2048, 1024], P(None, 'dev')
- w_down: bfloat16 [1, 64, 1024, 2048], P(None, 'dev')
Outputs:
- output: bfloat16 [512, 2048], P(('inst', 'dev'))
All inputs are finite; a program needn't handle non-finite values.
Results may differ from a plain program's by a relative error of at most 0.0163462.
Values are sent between devices in bfloat16 or wider.
A program may use at most 2.75 GiB of HBM per device.

v0:
```python
import jax
import jax.numpy as jnp
from jax import lax
from jax.sharding import PartitionSpec as P

NORM_EPS = 1e-6
ROPE_BASE = 10000.0


def rms_norm(in_rows, norm_gain):
    rows_f = in_rows.astype(jnp.float32)
    inv_rms = lax.rsqrt(jnp.mean(rows_f * rows_f, axis=-1, keepdims=True) + NORM_EPS)
    return (rows_f * inv_rms * norm_gain).astype(jnp.bfloat16)


def rotate_pos(in_vecs, positions):
    half_dim = in_vecs.shape[-1] // 2
    inv_freq = ROPE_BASE ** (-jnp.arange(half_dim, dtype=jnp.float32) * 2.0 / in_vecs.shape[-1])
    angles = positions.astype(jnp.float32)[:, None] * inv_freq[None, :]
    cosine = jnp.cos(angles)[:, None, :]
    sine_part = jnp.sin(angles)[:, None, :]
    first_half = in_vecs[..., :half_dim]
    second = in_vecs[..., half_dim:]
    return jnp.concatenate([first_half * cosine - second * sine_part, second * cosine + first_half * sine_part], axis=-1)


def attend(in_rows, key_cache, val_cache, lens_blk, w_query, w_keyval, w_out):
    tokens = in_rows.shape[0]
    kv_heads = key_cache.shape[1]
    seq_len = key_cache.shape[2]
    head_dim = key_cache.shape[3]
    q_heads = w_query.shape[1] // head_dim
    groups = q_heads // kv_heads
    q_rows = jnp.dot(in_rows, w_query, preferred_element_type=jnp.float32).astype(jnp.bfloat16)
    fresh_kv = jnp.dot(in_rows, w_keyval, preferred_element_type=jnp.float32).astype(jnp.bfloat16).reshape(tokens, 2, kv_heads, head_dim)
    q_rows = rotate_pos(q_rows.astype(jnp.float32).reshape(tokens, q_heads, head_dim), lens_blk).astype(jnp.bfloat16).reshape(tokens, kv_heads, groups, head_dim)
    new_key = rotate_pos(fresh_kv[:, 0].astype(jnp.float32), lens_blk).astype(jnp.bfloat16)
    new_val = fresh_kv[:, 1]
    score_scale = head_dim ** -0.5
    scores = jnp.einsum('tkgd,tksd->tkgs', q_rows, key_cache, preferred_element_type=jnp.float32) * score_scale
    valid_mask = jnp.arange(seq_len)[None, None, None, :] < lens_blk[:, None, None, None]
    scores = jnp.where(valid_mask, scores, -jnp.inf)
    self_score = jnp.einsum('tkgd,tkd->tkg', q_rows, new_key, preferred_element_type=jnp.float32) * score_scale
    peak_score = jnp.maximum(jnp.max(scores, axis=-1), self_score)
    weights = jnp.exp(scores - peak_score[..., None])
    self_weight = jnp.exp(self_score - peak_score)
    denom_sum = jnp.sum(weights, axis=-1) + self_weight
    prob_bf = (weights / denom_sum[..., None]).astype(jnp.bfloat16)
    self_prob = (self_weight / denom_sum).astype(jnp.bfloat16)
    context = jnp.einsum('tkgs,tksd->tkgd', prob_bf, val_cache, preferred_element_type=jnp.float32)
    context = context + self_prob.astype(jnp.float32)[..., None] * new_val.astype(jnp.float32)[:, :, None, :]
    context = context.astype(jnp.bfloat16).reshape(tokens, q_heads * head_dim)
    return jnp.dot(context, w_out, preferred_element_type=jnp.float32)


def dense_swiglu(in_rows, gate_w, up_w, down_w):
    act_gate = jnp.dot(in_rows, gate_w, preferred_element_type=jnp.float32)
    act_up = jnp.dot(in_rows, up_w, preferred_element_type=jnp.float32)
    inner_act = (jax.nn.silu(act_gate) * act_up).astype(jnp.bfloat16)
    return jnp.dot(inner_act, down_w, preferred_element_type=jnp.float32).astype(jnp.bfloat16)


def expert_swiglu(in_rows, gate_w, up_w, down_w):
    act_gate = jnp.einsum('secd,edf->secf', in_rows, gate_w, preferred_element_type=jnp.float32)
    act_up = jnp.einsum('secd,edf->secf', in_rows, up_w, preferred_element_type=jnp.float32)
    inner_act = (jax.nn.silu(act_gate) * act_up).astype(jnp.bfloat16)
    return jnp.einsum('secf,efd->secd', inner_act, down_w, preferred_element_type=jnp.float32).astype(jnp.bfloat16)


def capacity_of(block_rows, top_k, num_experts):
    per_block = block_rows * top_k
    return 2 * (per_block // num_experts) - 1 + min(1, per_block % num_experts)


def slot_of(ids_blk, num_experts):
    tokens, top_k = ids_blk.shape
    flat_ids = ids_blk.reshape(tokens * top_k)
    onehot = (flat_ids[:, None] == jnp.arange(num_experts)[None, :]).astype(jnp.int32)
    before = jnp.cumsum(onehot, axis=0) - onehot
    return jnp.sum(before * onehot, axis=1).reshape(tokens, top_k)


def gather_rows(in_rows, ids_blk, slot_blk, num_experts, capacity):
    tokens = in_rows.shape[0]
    expert_hit = (ids_blk[:, :, None] == jnp.arange(num_experts)[None, None, :]).astype(jnp.float32)
    slot_hit = (slot_blk[:, :, None] == jnp.arange(capacity)[None, None, :]).astype(jnp.float32)
    row_index = jnp.arange(tokens, dtype=jnp.float32)[:, None, None] * slot_hit
    owner_idx = jnp.einsum('tje,tjc->ec', expert_hit, row_index, precision=lax.Precision.HIGHEST)
    filled = jnp.einsum('tje,tjc->ec', expert_hit, slot_hit, precision=lax.Precision.HIGHEST)
    picked = jnp.take(in_rows, owner_idx.astype(jnp.int32), axis=0)
    return jnp.where(filled[:, :, None] > 0.5, picked, jnp.zeros_like(picked))


def combine_rows(expert_res, ids_blk, slot_blk, gates_blk):
    num_experts, capacity, model_dim = expert_res.shape
    flat_res = expert_res.reshape(num_experts * capacity, model_dim)
    picked = jnp.take(flat_res, ids_blk * capacity + slot_blk, axis=0)
    return jnp.sum(gates_blk[:, :, None] * picked.astype(jnp.float32), axis=1)


def solution(mesh):
    num_dev = mesh.shape['dev']
    half_side = mesh.shape['side'] // 2
    batch_spec = P(('inst', 'dev'))
    layer_batch = P(None, ('inst', 'dev'))
    expert_spec = P(None, 'dev')
    to_expert = [(column, column + half_side) for column in range(half_side)]
    to_attn = [(column + half_side, column) for column in range(half_side)]

    def device_fn(hidden, k_cache, v_cache, cache_lens, expert_ids, route_gates, attn_gain, ffn_gain, w_q, w_kv, w_o, shared_gate, shared_up, shared_down, w_gate, w_up, w_down):
        side_idx = lax.axis_index('side')
        is_attn = side_idx < half_side
        block_rows = hidden.shape[0] // half_side
        model_dim = hidden.shape[1]
        top_k = expert_ids.shape[2]
        local_experts = w_gate.shape[1]
        num_experts = local_experts * num_dev
        capacity = capacity_of(block_rows, top_k, num_experts)
        row_start = (side_idx % half_side) * block_rows
        x_state = lax.dynamic_slice_in_dim(hidden, row_start, block_rows, axis=0)
        lens_blk = lax.dynamic_slice_in_dim(cache_lens, row_start, block_rows, axis=0)

        def attn_stage(layer_ops):
            cur_rows, key_blk, val_blk, ids_blk, slot_blk, gain_a, gain_f, wq_l, wkv_l, wo_l, sg_l, su_l, sd_l = layer_ops
            normed = rms_norm(cur_rows, gain_a)
            mid_rows = (cur_rows.astype(jnp.float32) + attend(normed, key_blk, val_blk, lens_blk, wq_l, wkv_l, wo_l)).astype(jnp.bfloat16)
            ffn_in = rms_norm(mid_rows, gain_f)
            base_sum = mid_rows.astype(jnp.float32) + dense_swiglu(ffn_in, sg_l, su_l, sd_l).astype(jnp.float32)
            return base_sum, gather_rows(ffn_in, ids_blk, slot_blk, num_experts, capacity)

        def attn_skip(layer_ops):
            return jnp.zeros((block_rows, model_dim), jnp.float32), jnp.zeros((num_experts, capacity, model_dim), jnp.bfloat16)

        def expert_stage(expert_ops):
            return expert_swiglu(expert_ops[0], expert_ops[1], expert_ops[2], expert_ops[3])

        def expert_skip(expert_ops):
            return jnp.zeros_like(expert_ops[0])

        for layer_idx in range(k_cache.shape[0]):
            ids_blk = lax.dynamic_slice_in_dim(expert_ids[layer_idx], row_start, block_rows, axis=0)
            gates_blk = lax.dynamic_slice_in_dim(route_gates[layer_idx], row_start, block_rows, axis=0)
            slot_blk = slot_of(ids_blk, num_experts)
            key_blk = lax.dynamic_slice_in_dim(k_cache[layer_idx], row_start, block_rows, axis=0)
            val_blk = lax.dynamic_slice_in_dim(v_cache[layer_idx], row_start, block_rows, axis=0)
            layer_ops = (x_state, key_blk, val_blk, ids_blk, slot_blk, attn_gain[layer_idx], ffn_gain[layer_idx], w_q[layer_idx], w_kv[layer_idx], w_o[layer_idx], shared_gate[layer_idx], shared_up[layer_idx], shared_down[layer_idx])
            base_sum, send_buf = lax.cond(is_attn, attn_stage, attn_skip, layer_ops)
            spread = lax.all_to_all(send_buf.reshape(num_dev, local_experts, capacity, model_dim), 'dev', 0, 0)
            arrived = lax.ppermute(spread, 'side', to_expert)
            expert_res = lax.cond(is_attn, expert_skip, expert_stage, (arrived, w_gate[layer_idx], w_up[layer_idx], w_down[layer_idx]))
            back_buf = lax.ppermute(expert_res, 'side', to_attn)
            returned = lax.all_to_all(back_buf, 'dev', 0, 0).reshape(num_experts, capacity, model_dim)
            x_state = (base_sum + combine_rows(returned, ids_blk, slot_blk, gates_blk)).astype(jnp.bfloat16)
        gathered = lax.all_gather(x_state, 'side')
        return gathered[:half_side].reshape(half_side * block_rows, model_dim)

    in_specs = (batch_spec, layer_batch, layer_batch, batch_spec, layer_batch, layer_batch, P(), P(), P(), P(), P(), P(), P(), P(), expert_spec, expert_spec, expert_spec)
    return jax.shard_map(device_fn, mesh=mesh, in_specs=in_specs, out_specs=batch_spec, check_vma=False)
```

profile of v0, /device:TPU:0, one launch (start us, length us, event | category | flops | bytes accessed | tf_op | source)
XLA Modules:
  0.0 938.7 jit_solution(14344834800863662762)
XLA Ops:
  6.5 0.7 fusion.127
  7.2 0.7 constant_dynamic-slice_fusion
  8.2 0.4 copy-done.5
  8.7 18.0 %reduce-window.6 = s32[64,8,128]{2,1,0:T(8,128)S(1)} reduce-window(s32[64,8,128]{2,1,0:T(8,128)S(1)} %fusion.122, s32[]{:T(128)} %constant.130.clone.1), window={size=1x1x128 pad=0_0x0_0x127_0}, to_apply=%region_0.1 | reduce-window | flops 8323072 | bytes 524292 | tf_op jit(solution)/shard_map/reduce-window
  27.3 126.1 %conditional.2 = (f32[128,2048]{1,0:T(8,128)}, bf16[64,31,2048]{2,1,0:T(8,128)(2,1)}) conditional(s32[]{:T(128)} %convert_element_type.143, () %tuple.23, (bf16[256,2048]{1,0:T(8,128)(2,1)}, s32[]{:T(128)}, s32[256]{0:T(256)}, f32[1,2048]{1,0:T(1,128)}, bf16[1,2048,2048]{2,1,0:T(8,128)(2,1)}, /*index=5*/bf16[1,256,16,128,128]{4,3,2,1,0:T(8,128)(2,1)}, ...), branch_computations={%region_3.4_spmd, %region_4.9_spmd} | conditional | flops 6094735872 | bytes 315632640 | solution.py:147
  27.4 1.5 fusion.77
  28.9 8.6 fusion.66
  37.5 0.2 copy.114
  38.0 0.3 multiply_cosine_fusion
  38.3 0.5 copy-done.2
  38.8 1.3 fusion.63
  40.1 0.2 copy.113
  40.3 1.6 subtract_convert_fusion
  41.9 0.3 fusion.105
  42.2 40.0 %fusion.20 = f32[128,16,1,128]{3,2,1,0:T(1,128)S(1)} fusion(bf16[1,256,16,128,128]{4,3,2,1,0:T(8,128)(2,1)} %get-tuple-element.173, s32[]{:T(128)} %get-tuple-element.135, bf16[128,16,128,1]{2,1,0,3:T(8,128)(2,1)S(1)} %fusion.105), kind=kOutput, calls=%fused_computation.20 | convolution fusion | flops 67108864 | bytes 68682240 | tf_op jit(solution)/shard_map/cond/branch_1_fun/tkgd,tksd->tkgs/dot_general | solution.py:40
  82.2 2.2 fusion.82
  84.5 0.7 fusion.86
  85.2 0.7 fusion.97
  86.0 25.5 %fusion.18 = f32[128,16,1,128]{3,2,1,0:T(1,128)S(1)} fusion(bf16[1,256,16,128,128]{4,3,2,1,0:T(8,128)(2,1)} %get-tuple-element.175, s32[]{:T(128)} %get-tuple-element.135, bf16[128,16,128,1]{2,1,0,3:T(8,128)(2,1)S(1)} %fusion.97), kind=kOutput, calls=%fused_computation.18 | convolution fusion | flops 67108864 | bytes 68682240 | tf_op jit(solution)/shard_map/cond/branch_1_fun/tkgs,tksd->tkgd/dot_general | solution.py:50
  111.5 0.4 fusion.81
  111.9 5.1 multiply_reduce_fusion
  117.0 0.2 multiply_convert_fusion
  117.2 0.7 fusion.37
  117.9 5.9 fusion.60
  124.0 0.3 compare_and_fusion
  124.5 10.9 %gather_fusion = bf16[1984,2048]{1,0:T(8,128)(2,1)} fusion(bf16[128,2048]{1,0:T(8,128)(2,1)S(1)} %multiply_convert_fusion, s32[2048]{0:T(1024)S(1)} %pad_clamp_fusion), kind=kCustom, calls=%fused_computation | custom fusion | bytes 16260864 | tf_op jit(solution)/shard_map/cond/branch_1_fun/jit(_take)/gather | solution.py:90
  135.4 9.7 %reshape.269 = bf16[64,31,2048]{2,1,0:T(8,128)(2,1)} reshape(bf16[1984,2048]{1,0:T(8,128)(2,1)} %gather_fusion) | data formatting | bytes 16252928 | tf_op jit(solution)/shard_map/cond/branch_1_fun/jit(_take)/gather | solution.py:90
  145.2 0.2 fusion.76
  145.5 7.4 select_select_fusion
  153.4 11.1 %copy.94 = bf16[2,32,31,2048]{3,1,2,0:T(8,128)(2,1)} copy(bf16[2,32,31,2048]{3,2,1,0:T(8,128)(2,1)} %bitcast.37) | data formatting | bytes 16252928 | tf_op jit(solution)/shard_map/reshape | solution.py:148
  164.5 95.7 %all_to_all.10 = bf16[2,32,31,2048]{3,1,2,0:T(8,128)(2,1)S(1)} all-to-all(bf16[2,32,31,2048]{3,1,2,0:T(8,128)(2,1)} %copy.94), channel_id=1, replica_groups=mesh['inst'=1,'dev'=2,'side'=4] {'dev'}, dimensions={0} | all-to-all | bytes 16252928 | tf_op jit(solution)/shard_map/all_to_all | solution.py:148
  260.2 4.4 collective-permute-start
  264.7 170.5 %collective-permute-done = bf16[2,32,31,2048]{3,1,2,0:T(8,128)(2,1)} collective-permute-done((bf16[2,32,31,2048]{3,1,2,0:T(8,128)(2,1)S(1)}, bf16[2,32,31,2048]{3,1,2,0:T(8,128)(2,1)}, u32[]{:S(2)}, u32[]{:S(2)}) %collective-permute-start) | collective-permute-done | bytes 8126496 | tf_op jit(solution)/shard_map/ppermute | solution.py:149
  435.2 4.6 conditional.3
  435.3 4.3 broadcast.222
  439.8 11.2 %copy.96 = bf16[2,32,31,2048]{3,1,2,0:T(8,128)(2,1)} copy(bf16[2,32,31,2048]{3,2,0,1:T(8,128)(2,1)} %get-tuple-element.270) | data formatting | bytes 16252928 | tf_op jit(solution)/shard_map/cond | solution.py:150
  451.0 1.4 collective-permute-start.1
  452.4 321.3 %collective-permute-done.1 = bf16[2,32,31,2048]{3,1,2,0:T(8,128)(2,1)} collective-permute-done((bf16[2,32,31,2048]{3,1,2,0:T(8,128)(2,1)}, bf16[2,32,31,2048]{3,1,2,0:T(8,128)(2,1)}, u32[]{:S(2)}, u32[]{:S(2)}) %collective-permute-start.1) | collective-permute-done | bytes 8126496 | tf_op jit(solution)/shard_map/ppermute | solution.py:151
  773.7 6.9 all-to-all-start.1
  780.6 0.3 all-gather.3.cloned.1.call-start
  781.6 87.6 %all-to-all-done.1 = bf16[2,32,31,2048]{3,1,2,0:T(8,128)(2,1)} async-done(((bf16[2,32,31,2048]{3,1,2,0:T(8,128)(2,1)}), bf16[2,32,31,2048]{3,1,2,0:T(8,128)(2,1)}, u32[]{:S(2)}, u32[]{:S(2)}) %all-to-all-start.1) | async-done | bytes 8126496 | tf_op jit(solution)/shard_map/all_to_all | solution.py:152
  869.2 11.0 %copy.97 = bf16[2,32,31,2048]{3,2,1,0:T(8,128)(2,1)} copy(bf16[2,32,31,2048]{3,1,2,0:T(8,128)(2,1)} %all-to-all-done.1) | data formatting | bytes 16252928 | tf_op jit(solution)/shard_map/all_to_all | solution.py:152
  880.2 9.7 %reshape_reshape.3 = bf16[1984,2048]{1,0:T(8,128)(2,1)} reshape(bf16[2,32,31,2048]{3,2,1,0:T(8,128)(2,1)} %copy.97) | data formatting | bytes 16252928 | tf_op jit(solution)/shard_map/reshape;reshape | solution.py:96
  890.0 13.2 %gather_fusion.1 = bf16[1024,2048]{1,0:T(8,128)(2,1)} fusion(bf16[1984,2048]{1,0:T(8,128)(2,1)} %reshape_reshape.3, s32[1024]{0:T(1024)S(1)} %broadcast_clamp_fusion), kind=kCustom, calls=%fused_computation.1 | custom fusion | bytes 8392704 | tf_op jit(solution)/shard_map/jit(_take)/gather | solution.py:97
  903.1 5.6 multiply_reduce_fusion.1
  908.7 2.2 add_convert_fusion.2
  910.9 18.3 %all-gather.3.cloned.1.call-done = bf16[512,2048]{1,0:T(8,128)(2,1)} async-done(((bf16[128,2048]{1,0:T(8,128)(2,1)}), bf16[512,2048]{1,0:T(8,128)(2,1)}) %all-gather.3.cloned.1.call-update) | async-done | bytes 2097168 | tf_op jit(solution)/shard_map/all_gather | solution.py:154
  929.3 2.3 slice.55
  (62 shorter events, 2.5 us)
Async XLA Ops:
  6.5 774.7 %copy-start = (f32[1,256,8]{1,2,0:T(8,128)S(1)}, f32[1,256,8]{1,2,0:T(8,128)}, u32[]{:S(2)}) copy-start(f32[1,256,8]{1,2,0:T(8,128)} %param.26) | copy-start | bytes 24580
  8.0 0.6 copy-start.5
  27.3 11.4 %slice-start = ((s8[8388608]{0:T(1024)(128)(4,1)}), s8[4194304]{0:T(1024)(128)(4,1)S(1)}, s32[]{:S(2)}) async-start(s8[8388608]{0:T(1024)(128)(4,1)} %bitcast.177), calls=%async_computation.3 | async-start | bytes 8388608 | tf_op jit(solution)/shard_map/cond
  28.8 9.0 copy-start.10
  28.8 9.9 %slice-start.1 = ((s8[8388608]{0:T(1024)(128)(4,1)}), s8[4194304]{0:T(1024)(128)(4,1)S(1)}, s32[]{:S(2)}) async-start(s8[8388608]{0:T(1024)(128)(4,1)} %bitcast.177), calls=%async_computation.4 | async-start | bytes 8388608 | tf_op jit(solution)/shard_map/cond
  28.9 9.9 %copy-start.4 = (bf16[256,2048]{1,0:T(8,128)(2,1)S(1)}, bf16[256,2048]{1,0:T(8,128)(2,1)}, u32[]{:S(2)}) copy-start(bf16[256,2048]{1,0:T(8,128)(2,1)} %get-tuple-element.169) | copy-start | bytes 3145732 | tf_op jit(solution)/shard_map/cond
  28.9 9.9 %copy-start.7 = (f32[1,2048]{1,0:T(1,128)S(1)}, f32[1,2048]{1,0:T(1,128)}, u32[]{:S(2)}) copy-start(f32[1,2048]{1,0:T(1,128)} %get-tuple-element.171) | copy-start | bytes 24580 | tf_op jit(solution)/shard_map/cond
  37.8 1.0 copy-start.2
  86.0 25.5 %copy-start.3 = (bf16[16,8,32,128]{3,2,1,0:T(8,128)(2,1)S(1)}, bf16[16,8,32,128]{3,2,1,0:T(8,128)(2,1)}, u32[]{:S(2)}) copy-start(bf16[16,8,32,128]{3,2,1,0:T(8,128)(2,1)} %copy-done.2) | copy-start | bytes 3145732 | tf_op jit(solution)/shard_map/cond
  111.5 5.5 copy-start.9
  111.9 5.3 copy-start.1
  260.2 174.9 %collective-permute-start = (bf16[2,32,31,2048]{3,1,2,0:T(8,128)(2,1)S(1)}, bf16[2,32,31,2048]{3,1,2,0:T(8,128)(2,1)}, u32[]{:S(2)}, u32[]{:S(2)}) collective-permute-start(bf16[2,32,31,2048]{3,1,2,0:T(8,128)(2,1)S(1)} %all_to_all.10), channel_id=1, source_target_pairs={{0,2},{1,3},{4,6},{5,7}} | collective-permute-start | bytes 24379400 | tf_op jit(solution)/shard_map/ppermute | solution.py:149
  451.0 330.1 %copy-start.6 = (s32[1,128,8]{2,1,0:T(8,128)S(1)}, s32[1,128,8]{2,1,0:T(8,128)}, u32[]{:S(2)}) copy-start(s32[1,128,8]{2,1,0:T(8,128)} %copy-done.5) | copy-start | bytes 12292
  451.0 330.4 %copy-start.8 = (s32[1,256,8]{1,2,0:T(8,128)S(1)}, s32[1,256,8]{1,2,0:T(8,128)}, u32[]{:S(2)}) copy-start(s32[1,256,8]{1,2,0:T(8,128)} %param.25) | copy-start | bytes 24580
  451.0 322.8 %collective-permute-start.1 = (bf16[2,32,31,2048]{3,1,2,0:T(8,128)(2,1)}, bf16[2,32,31,2048]{3,1,2,0:T(8,128)(2,1)}, u32[]{:S(2)}, u32[]{:S(2)}) collective-permute-start(bf16[2,32,31,2048]{3,1,2,0:T(8,128)(2,1)} %copy.96), channel_id=1, source_target_pairs={{2,0},{3,1},{6,4},{7,5}} | collective-permute-start | bytes 24379400 | tf_op jit(solution)/shard_map/ppermute | solution.py:151
  773.7 95.5 %all-to-all-start.1 = ((bf16[2,32,31,2048]{3,1,2,0:T(8,128)(2,1)}), bf16[2,32,31,2048]{3,1,2,0:T(8,128)(2,1)}, u32[]{:S(2)}, u32[]{:S(2)}) async-start(bf16[2,32,31,2048]{3,1,2,0:T(8,128)(2,1)} %collective-permute-done.1), calls=%async_computation.1 | async-start | bytes 16252928 | tf_op jit(solution)/shard_map/all_to_all | solution.py:152
  780.6 148.6 %all-gather.3.cloned.1.call-start = ((), (), s32[]{:S(2)}) async-start(), calls=%async_computation.2 | async-start | bytes 2621440 | tf_op jit(solution)/shard_map/all_gather | solution.py:154
Sparse Core Ops, SparseCore 0:
  911.1 18.1 all-gather.2
where the time goes:
time: 945 us; the launch traced here: 939 us
  waiting for transfers between devices  598 us (63%)
  blocking collectives  95.7 us (10%)
  local copies, waits for them, and re-layouts  88 us (9%)
  matrix products  87.6 us (9%)
  other arithmetic  41.6 us (4%)
  between operations  13.8 us (1%)
  starting transfers between devices  13 us (1%)
    ppermute x1, waiting for transfers between devices, device_fn(): back_buf = lax.ppermute(expert_res, 'side', to_attn)  321 us
    ppermute x1, waiting for transfers between devices, device_fn(): arrived = lax.ppermute(spread, 'side', to_expert)  170 us
    all_to_all x1, blocking collectives, device_fn(): lax.all_to_all(send_buf.reshape(num_dev, local_experts, capacity, model_d...  95.7 us
    all_to_all x1, waiting for transfers between devices, device_fn(): lax.all_to_all(back_buf, 'dev', 0, 0)  87.6 us
    dot_general x1, matrix products, attend(): jnp.einsum('tkgd,tksd->tkgs', q_rows, key_cache, preferred_element_type=j...  40 us
    dot_general x1, matrix products, attend(): jnp.einsum('tkgs,tksd->tkgd', prob_bf, val_cache, preferred_element_type=...  25.5 us
    gather x2, local copies, waits for them, and re-layouts, gather_rows(): picked = jnp.take(in_rows, owner_idx.astype(jnp.int32), axis=0)  20.6 us
    another operation x4, other arithmetic  19.8 us
  transfers between devices with their start and end apart: 4, of which 4 were waited for; matrix products, arithmetic and copies ran while one was open for 0% of the time, Pallas kernels for 0%

commit v1 on v0

v1 whole, which is shorter than its diff:
```python
import functools

import numpy as np
import jax
import jax.numpy as jnp
from jax import lax
from jax.experimental import pallas as pl
from jax.experimental.pallas import tpu as pltpu
from jax.sharding import PartitionSpec as P

NORM_EPS = 1e-6
ROPE_BASE = 10000.0
MESH = pl.DeviceIdType.MESH
F32 = jnp.float32
BF16 = jnp.bfloat16

ROWS = 128
HEADS = 8
HD = 128
DIM = 2048
HALF = DIM // 2
GROUP = 8
KV_RING = 4
RING = 16
EXPERTS = 16
SLOTS = 32
CHUNKS = 4
CW = HALF // CHUNKS
FIRST_AXIS = (1, 0, 1, 1)


def norm_rows(rows_f, gain):
    inv_rms = lax.rsqrt(jnp.mean(rows_f * rows_f, axis=-1, keepdims=True) + NORM_EPS)
    return (rows_f * inv_rms * gain).astype(BF16)


def attn_kernel(lens_ref, hidden_ref, gain_ref, freq_ref, wq_ref, wkv_ref, kc_ref, vc_ref, ctx_ref,
                xbuf, wbuf, pos_buf, q3, k3, v3, c3, sbuf, kbuf, vbuf, xsem, wsem, ksem, vsem):
    side = lax.axis_index('side')
    row0 = (side // 2) * ROWS
    core = side % 2
    h0 = core * HEADS
    groups = ROWS // GROUP

    def kv_copies(tok, slot):
        size = pl.multiple_of(((lens_ref[row0 + tok] + 15) // 16) * 16, 16)
        k_cp = pltpu.make_async_copy(kc_ref.at[0, row0 + tok, pl.ds(h0, HEADS), pl.ds(0, size), :],
                                     kbuf.at[slot, :, pl.ds(0, size), :], ksem.at[slot])
        v_cp = pltpu.make_async_copy(vc_ref.at[0, row0 + tok, pl.ds(h0, HEADS), pl.ds(0, size), :],
                                     vbuf.at[slot, :, pl.ds(0, size), :], vsem.at[slot])
        return k_cp, v_cp

    def start_group(grp):
        for i in range(GROUP):
            k_cp, v_cp = kv_copies(grp * GROUP + i, lax.rem(grp, KV_RING) * GROUP + i)
            k_cp.start()
            v_cp.start()

    x_cp = pltpu.make_async_copy(hidden_ref.at[pl.ds(row0, ROWS), :], xbuf, xsem)
    x_cp.start()
    w_cps = []
    for i in range(6):
        kind, j = i // 2, i % 2
        col = core * HALF + j * 512
        if kind == 0:
            src = wq_ref.at[0, :, pl.ds(col, 512)]
        else:
            src = wkv_ref.at[0, :, pl.ds((kind - 1) * DIM + col, 512)]
        cp = pltpu.make_async_copy(src, wbuf.at[i], wsem.at[i])
        cp.start()
        w_cps.append(cp)

    def zero_slot(i, carry):
        vbuf[i] = jnp.zeros((HEADS, HD, HD), BF16)
        return carry
    lax.fori_loop(0, KV_RING * GROUP, zero_slot, 0)

    start_group(jnp.int32(0))
    start_group(jnp.int32(1))

    def fill_pos(i, carry):
        pos_buf[pl.ds(i, 1), :] = jnp.full((1, HD), lens_ref[row0 + i].astype(F32), F32)
        return carry
    lax.fori_loop(0, ROWS, fill_pos, 0)
    angles = pos_buf[...] * freq_ref[...]
    cosine = jnp.cos(angles)
    lane = lax.broadcasted_iota(jnp.int32, (ROWS, HD), 1)
    sine = jnp.where(lane < HD // 2, -jnp.sin(angles), jnp.sin(angles))

    x_cp.wait()
    normed = norm_rows(xbuf[...].astype(F32), gain_ref[...])
    for i in range(6):
        kind, j = i // 2, i % 2
        w_cps[i].wait()
        res = jnp.dot(normed, wbuf[i], preferred_element_type=F32).astype(BF16).astype(F32)
        for hh in range(4):
            h = j * 4 + hh
            val = res[:, hh * HD:(hh + 1) * HD]
            if kind < 2:
                val = (val * cosine + pltpu.roll(val, HD // 2, 1) * sine).astype(BF16).astype(F32)
            (q3, k3, v3)[kind][:, h, :] = val
        if i == 1:
            start_group(jnp.int32(2))
        if i == 3:
            start_group(jnp.int32(3))

    row_id = lax.broadcasted_iota(jnp.int32, (HEADS, HD), 0)
    lane_id = lax.broadcasted_iota(jnp.int32, (HEADS, HD), 1)

    def wait_kv(grp, which):
        for i in range(GROUP):
            kv_copies(grp * GROUP + i, lax.rem(grp, KV_RING) * GROUP + i)[which].wait()

    def score_group(grp):
        for i in range(GROUP):
            tok = grp * GROUP + i
            slot = lax.rem(grp, KV_RING) * GROUP + i
            keys = kbuf[slot].reshape(HEADS * HD, HD)
            full = lax.dot_general(q3[tok].astype(BF16), keys, (((1,), (1,)), ((), ())), preferred_element_type=F32)
            sc = jnp.zeros((HEADS, HD), F32)
            for h in range(HEADS):
                sc = jnp.where(row_id == h, full[:, h * HD:(h + 1) * HD], sc)
            sbuf[lax.rem(grp, 2), i] = jnp.where(lane_id < lens_ref[row0 + tok], sc * (HD ** -0.5), -jnp.inf)

    def value_group(grp):
        for i in range(GROUP):
            tok = grp * GROUP + i
            slot = lax.rem(grp, KV_RING) * GROUP + i
            sc = sbuf[lax.rem(grp, 2), i]
            self_sc = jnp.sum(q3[tok] * k3[tok], axis=-1, keepdims=True) * (HD ** -0.5)
            peak = jnp.maximum(jnp.max(sc, axis=-1, keepdims=True), self_sc)
            wts = jnp.exp(sc - peak)
            self_w = jnp.exp(self_sc - peak)
            denom = jnp.sum(wts, axis=-1, keepdims=True) + self_w
            prob = wts / denom
            self_p = (self_w / denom).astype(BF16).astype(F32)
            wide = jnp.concatenate([jnp.where(row_id == h, prob, 0.0) for h in range(HEADS)], axis=1).astype(BF16)
            vals = vbuf[slot].reshape(HEADS * HD, HD)
            ctx = jnp.dot(wide, vals, preferred_element_type=F32)
            c3[tok] = ctx + self_p * v3[tok]

    wait_kv(jnp.int32(0), 0)
    score_group(jnp.int32(0))

    def body(grp, carry):
        wait_kv(grp, 1)
        wait_kv(grp + 1, 0)
        value_group(grp)
        score_group(grp + 1)

        @pl.when(grp + KV_RING < groups)
        def _():
            for i in range(GROUP):
                nxt = grp + KV_RING
                for cp in kv_copies(nxt * GROUP + i, lax.rem(nxt, KV_RING) * GROUP + i):
                    cp.start()
        return carry
    lax.fori_loop(0, groups - 1, body, 0)
    wait_kv(jnp.int32(groups - 1), 1)
    value_group(jnp.int32(groups - 1))
    for h in range(HEADS):
        ctx_ref[:, h * HD:(h + 1) * HD] = c3[:, h, :].astype(BF16)


def attention(hidden, lens, gain, w_q, w_kv, k_cache, v_cache):
    freq = ROPE_BASE ** (-np.arange(HD // 2, dtype=np.float64) * 2.0 / HD)
    freq = np.concatenate([freq, freq])[None, :].astype(np.float32)
    any_spec = pl.BlockSpec(memory_space=pl.ANY)
    vmem_spec = pl.BlockSpec(memory_space=pltpu.VMEM)
    slots = KV_RING * GROUP
    return pl.pallas_call(
        attn_kernel,
        out_shape=jax.ShapeDtypeStruct((ROWS, HALF), BF16),
        in_specs=[pl.BlockSpec(memory_space=pltpu.SMEM), any_spec, vmem_spec, vmem_spec] + [any_spec] * 4,
        out_specs=vmem_spec,
        scratch_shapes=[
            pltpu.VMEM((ROWS, DIM), BF16),
            pltpu.VMEM((6, DIM, 512), BF16),
            pltpu.VMEM((ROWS, HD), F32),
            pltpu.VMEM((ROWS, HEADS, HD), F32),
            pltpu.VMEM((ROWS, HEADS, HD), F32),
            pltpu.VMEM((ROWS, HEADS, HD), F32),
            pltpu.VMEM((ROWS, HEADS, HD), F32),
            pltpu.VMEM((2, GROUP, HEADS, HD), F32),
            pltpu.VMEM((slots, HEADS, HD, HD), BF16),
            pltpu.VMEM((slots, HEADS, HD, HD), BF16),
            pltpu.SemaphoreType.DMA,
            pltpu.SemaphoreType.DMA((6,)),
            pltpu.SemaphoreType.DMA((slots,)),
            pltpu.SemaphoreType.DMA((slots,)),
        ],
        compiler_params=pltpu.CompilerParams(vmem_limit_bytes=60 * 1024 * 1024),
        name='attend',
    )(lens, hidden, gain, jnp.asarray(freq), w_q, w_kv, k_cache, v_cache)


def moe_kernel(ctx_ref, rt_ref, gain_ref, hidden_ref, wo_ref, sg_ref, su_ref, sd_ref, wg_ref, wu_ref, wd_ref, out_ref,
               ring, ctx_sib, xbuf, mbuf, uall, ish, base, rt_all, dmat, cg, xe, inner, ybuf, pbuf, recv1, send2, recv2, oall,
               ring_sem, x_sem, misc_s, misc_r, u_s, u_r, uf_s, uf_r, in_s, in_r, p1_s, p1_r, p2_s, p2_r,
               os_s, os_r, ox_s, ox_r, of_s, of_r, out_sem):
    inst = lax.axis_index('inst')
    dy = lax.axis_index('dev')
    side = lax.axis_index('side')
    cx = side // 2
    core = side % 2
    blk0 = dy * 2 + cx
    col0 = core * HALF

    def dev_of(y, x, c):
        return (inst, y, x * 2 + c)
    sibling = dev_of(dy, cx, 1 - core)
    x_nbr = dev_of(dy, 1 - cx, core)
    y_nbr = dev_of(1 - dy, cx, core)
    diag = dev_of(1 - dy, 1 - cx, core)

    def rdma(src, dst, s_sem, r_sem, dev):
        return pltpu.make_async_remote_copy(src_ref=src, dst_ref=dst, send_sem=s_sem, recv_sem=r_sem,
                                            device_id=dev, device_id_type=MESH)

    def start_wo(j):
        pltpu.make_async_copy(wo_ref.at[0, :, pl.ds(col0 + j * 512, 512)], ring.at[j], ring_sem.at[j]).start()

    def start_gate(e, slot):
        pltpu.make_async_copy(wg_ref.at[0, cx * EXPERTS + e, :, pl.ds(core * 512, 512)], ring.at[slot], ring_sem.at[slot]).start()

    def start_up(e, slot):
        pltpu.make_async_copy(wu_ref.at[0, cx * EXPERTS + e, :, pl.ds(core * 512, 512)], ring.at[slot], ring_sem.at[slot]).start()

    def start_down(m, slot):
        k = m // 4
        g = m % 4
        for i in range(4):
            pltpu.make_async_copy(wd_ref.at[0, cx * EXPERTS + g * 4 + i, :, pl.ds(col0 + k * CW, CW)],
                                  ring.at[slot, pl.ds((i // 2) * 1024, 1024), pl.ds((i % 2) * CW, CW)],
                                  ring_sem.at[slot]).start()

    def wait_slot(slot):
        pltpu.make_async_copy(wg_ref.at[0, 0, :, pl.ds(0, 512)], ring.at[slot], ring_sem.at[slot]).wait()

    def start_gu_block(b):
        e, up = (b - 5) // 2, (b - 5) % 2
        (start_up if up else start_gate)(e, b % RING)

    x_cp = pltpu.make_async_copy(hidden_ref.at[pl.ds(cx * ROWS, ROWS), pl.ds(col0, HALF)], xbuf, x_sem)
    x_cp.start()
    start_wo(0)
    start_wo(1)
    pltpu.make_async_copy(sg_ref.at[0, :, pl.ds(core * 512, 512)], ring.at[2], ring_sem.at[2]).start()
    pltpu.make_async_copy(su_ref.at[0, :, pl.ds(core * 512, 512)], ring.at[3], ring_sem.at[3]).start()
    for j in range(2):
        pltpu.make_async_copy(sd_ref.at[0, :, pl.ds(col0 + j * 512, 512)], ring.at[4, pl.ds(j * 1024, 1024), :],
                              ring_sem.at[4]).start()
    for b in range(5, RING):
        start_gu_block(b)

    barrier = pltpu.get_barrier_semaphore()
    for dev in (sibling, x_nbr, y_nbr, diag):
        pl.semaphore_signal(barrier, inc=1, device_id=dev, device_id_type=MESH)
    pl.semaphore_wait(barrier, 4)

    ctx_cp = rdma(ctx_ref, ctx_sib, misc_s.at[0], misc_r.at[0], sibling)
    ctx_cp.start()
    rt_cp = rdma(rt_ref, rt_all.at[dy], misc_s.at[1], misc_r.at[1], y_nbr)
    rt_cp.start()
    rt_all[dy] = rt_ref[...]

    wait_slot(0)
    wait_slot(1)
    x_cp.wait()
    own_row = core * HALF
    sib_row = (1 - core) * HALF
    accs = [jnp.dot(ctx_ref[...], ring[j, pl.ds(own_row, HALF), :], preferred_element_type=F32) for j in range(2)]
    ctx_cp.wait_recv()
    for j in range(2):
        acc = accs[j] + jnp.dot(ctx_sib[...], ring[j, pl.ds(sib_row, HALF), :], preferred_element_type=F32)
        mbuf[core, :, j * 512:(j + 1) * 512] = (xbuf[:, j * 512:(j + 1) * 512].astype(F32) + acc).astype(BF16)
    start_gu_block(16)
    start_gu_block(17)
    m_cp = rdma(mbuf.at[core], mbuf.at[core], misc_s.at[2], misc_r.at[2], sibling)
    m_cp.start()
    rdma(mbuf.at[1 - core], mbuf.at[1 - core], misc_s.at[2], misc_r.at[2], sibling).wait_recv()
    m_lo = mbuf[0].astype(F32)
    m_hi = mbuf[1].astype(F32)
    total = jnp.sum(m_lo * m_lo, axis=-1, keepdims=True) + jnp.sum(m_hi * m_hi, axis=-1, keepdims=True)
    inv_rms = lax.rsqrt(total / DIM + NORM_EPS)
    uall[blk0, :, 0:HALF] = (m_lo * inv_rms * gain_ref[:, 0:HALF]).astype(BF16)
    uall[blk0, :, HALF:DIM] = (m_hi * inv_rms * gain_ref[:, HALF:DIM]).astype(BF16)

    def u_part(b, c):
        return uall.at[b, pl.ds(c * 64, 64), :]
    u_cps = [rdma(u_part(blk0, core), u_part(blk0, core), u_s.at[r], u_r.at[r], dev)
             for r, dev in enumerate((x_nbr, y_nbr, diag))]
    for r in (2, 1, 0):
        u_cps[r].start()

    wait_slot(2)
    wait_slot(3)
    u_own = uall[blk0]
    gate = jnp.dot(u_own, ring[2], preferred_element_type=F32)
    up = jnp.dot(u_own, ring[3], preferred_element_type=F32)
    ish[core] = (jax.nn.silu(gate) * up).astype(BF16)
    start_gu_block(18)
    start_gu_block(19)
    ish_cp = rdma(ish.at[core], ish.at[core], misc_s.at[3], misc_r.at[3], sibling)
    ish_cp.start()

    rt_cp.wait_send()
    rdma(rt_all.at[1 - dy], rt_all.at[1 - dy], misc_s.at[1], misc_r.at[1], y_nbr).wait_recv()
    expert_id = (dy * 32 + cx * EXPERTS + lax.broadcasted_iota(jnp.int32, (EXPERTS, ROWS), 0)).astype(F32)
    before = (lax.broadcasted_iota(jnp.int32, (ROWS, ROWS), 0) < lax.broadcasted_iota(jnp.int32, (ROWS, ROWS), 1))
    before = jnp.where(before, 1.0, 0.0).astype(BF16)
    slot_id = lax.broadcasted_iota(jnp.int32, (SLOTS, ROWS), 0).astype(F32)
    for yb in range(2):
        for xb in range(2):
            b = yb * 2 + xb
            hit = jnp.zeros((EXPERTS, ROWS), F32)
            wts = jnp.zeros((EXPERTS, ROWS), F32)
            for j in range(8):
                same = rt_all[yb, j:j + 1, xb * ROWS:(xb + 1) * ROWS] == expert_id
                hit = jnp.where(same, 1.0, hit)
                wts = jnp.where(same, rt_all[yb, 8 + j:9 + j, xb * ROWS:(xb + 1) * ROWS], wts)
            place = jnp.dot(hit.astype(BF16), before, preferred_element_type=F32)
            place = jnp.where(hit > 0.5, place, -1.0)
            pieces = []
            for e in range(EXPERTS):
                match = place[e:e + 1, :] == slot_id
                dmat[b, e * SLOTS:(e + 1) * SLOTS, :] = jnp.where(match, 1.0, 0.0).astype(BF16)
                pieces.append(jnp.where(match, wts[e:e + 1, :], 0.0))
            for q in range(4):
                part = jnp.concatenate(pieces[q * 4:(q + 1) * 4], axis=0).T
                high = part.astype(BF16)
                rest = part - high.astype(F32)
                mid = rest.astype(BF16)
                low = (rest - mid.astype(F32)).astype(BF16)
                cg[b, 0:128, q * 128:(q + 1) * 128] = high
                cg[b, 128:256, q * 128:(q + 1) * 128] = mid
                cg[b, 256:384, q * 128:(q + 1) * 128] = low

    def dispatch(b):
        def one(n, carry):
            cols = pl.ds(pl.multiple_of(n * 512, 512), 512)
            rows = jnp.dot(dmat[b], uall[b, :, cols], preferred_element_type=F32).astype(BF16)
            for e in range(EXPERTS):
                xe[e, pl.ds(pl.multiple_of(b * SLOTS, SLOTS), SLOTS), cols] = rows[e * SLOTS:(e + 1) * SLOTS, :]
            return carry
        lax.fori_loop(0, DIM // 512, one, 0)

    dispatch(blk0)
    rdma(ish.at[1 - core], ish.at[1 - core], misc_s.at[3], misc_r.at[3], sibling).wait_recv()
    wait_slot(4)
    for j in range(2):
        acc = jnp.dot(ish[0], ring[4, j * 1024:j * 1024 + 512, :], preferred_element_type=F32)
        acc = acc + jnp.dot(ish[1], ring[4, j * 1024 + 512:(j + 1) * 1024, :], preferred_element_type=F32)
        base[:, j * 512:(j + 1) * 512] = mbuf[core, :, j * 512:(j + 1) * 512].astype(F32) + acc.astype(BF16).astype(F32)
    start_gu_block(20)

    blk_of = (dy * 2 + 1 - cx, (1 - dy) * 2 + cx, (1 - dy) * 2 + 1 - cx)
    fwd = []
    for r in (1, 0, 2):
        b = blk_of[r]
        rdma(u_part(b, core), u_part(b, core), u_s.at[r], u_r.at[r], sibling).wait_recv()
        cp = rdma(u_part(b, core), u_part(b, core), uf_s.at[r], uf_r.at[r], sibling)
        cp.start()
        fwd.append(cp)
        rdma(u_part(b, 1 - core), u_part(b, 1 - core), uf_s.at[r], uf_r.at[r], sibling).wait_recv()
        dispatch(b)

    def in_part(e, c):
        return inner.at[e, :, pl.ds(pl.multiple_of(c * 512, 512), 512)]

    def expert_up(e):
        slot_g = lax.rem(5 + 2 * e, RING)
        slot_u = lax.rem(6 + 2 * e, RING)
        wait_slot(slot_g)
        wait_slot(slot_u)
        rows = xe[e]
        gate = jnp.dot(rows, ring[slot_g], preferred_element_type=F32)
        up = jnp.dot(rows, ring[slot_u], preferred_element_type=F32)
        inner[e, :, pl.ds(pl.multiple_of(core * 512, 512), 512)] = (jax.nn.silu(gate) * up).astype(BF16)
        rdma(in_part(e, core), in_part(e, core), in_s.at[e], in_r.at[e], sibling).start()
        return slot_g, slot_u

    def first_half(e, carry):
        slot_g, slot_u = expert_up(e)
        start_gate(e + 8, slot_g)
        start_up(e + 8, slot_u)
        return carry
    lax.fori_loop(0, 8, first_half, 0)

    def second_half(e, carry):
        slot_g, slot_u = expert_up(e)
        start_down(2 * (e - 8), slot_g)
        start_down(2 * (e - 8) + 1, slot_u)
        return carry
    lax.fori_loop(8, 16, second_half, 0)

    def block_at(y, x):
        return y * 2 + x

    def stage1(k):
        axis = FIRST_AXIS[k]
        if axis == 1:
            far, near = block_at(1 - dy, 1 - cx), block_at(1 - dy, cx)
            dev = y_nbr
        else:
            far, near = block_at(1 - dy, 1 - cx), block_at(dy, 1 - cx)
            dev = x_nbr
        return [rdma(pbuf.at[k, b], recv1.at[k, i], p1_s.at[k, i], p1_r.at[k, i], dev) for i, b in enumerate((far, near))]

    def stage2(k):
        axis = FIRST_AXIS[k]
        dev = x_nbr if axis == 1 else y_nbr
        return rdma(send2.at[k], recv2.at[k], p2_s.at[k], p2_r.at[k], dev)

    def run_stage2(k):
        axis = FIRST_AXIS[k]
        b = block_at(dy, 1 - cx) if axis == 1 else block_at(1 - dy, cx)
        stage1(k)[0].wait_recv()
        send2[k] = pbuf[k, b] + recv1[k, 0]
        stage2(k).start()

    def o_part(x, c, k):
        return oall.at[x, c, k]

    def run_final(k):
        stage1(k)[1].wait_recv()
        stage2(k).wait_recv()
        routed = pbuf[k, blk0] + recv1[k, 1] + recv2[k]
        oall[cx, core, k] = (base[:, k * CW:(k + 1) * CW] + routed).astype(BF16)
        mine = o_part(cx, core, k)
        rdma(mine, mine, os_s.at[k], os_r.at[k], sibling).start()
        rdma(mine, mine, ox_s.at[k], ox_r.at[k], x_nbr).start()
        store_out(cx, core, k, 0).start()

    def store_out(x, c, k, which):
        return pltpu.make_async_copy(o_part(x, c, k),
                                     out_ref.at[pl.ds(x * ROWS, ROWS), pl.ds(pl.multiple_of(c * HALF + k * CW, CW), CW)],
                                     out_sem.at[which, k])

    def run_forward(k):
        theirs = o_part(1 - cx, core, k)
        rdma(theirs, theirs, ox_s.at[k], ox_r.at[k], x_nbr).wait_recv()
        rdma(theirs, theirs, of_s.at[k], of_r.at[k], sibling).start()
        store_out(1 - cx, core, k, 1).start()

    for e in range(EXPERTS):
        rdma(in_part(e, 1 - core), in_part(e, 1 - core), in_s.at[e], in_r.at[e], sibling).wait_recv()

    for k in range(CHUNKS):
        def down_group(g, carry):
            slot = lax.rem(5 + 4 * k + g, RING)
            wait_slot(slot)
            for i in range(4):
                e = g * 4 + i
                w = ring[slot, (i // 2) * 1024:(i // 2 + 1) * 1024, (i % 2) * CW:(i % 2 + 1) * CW]
                res = jnp.dot(inner[e], w, preferred_element_type=F32).astype(BF16)
                for b in range(4):
                    ybuf[b, pl.ds(pl.multiple_of(e * SLOTS, SLOTS), SLOTS), :] = res[b * SLOTS:(b + 1) * SLOTS, :]
            return carry
        lax.fori_loop(0, 4, down_group, 0)

        def combine(b, carry):
            res = jnp.dot(cg[b], ybuf[b], preferred_element_type=F32)
            pbuf[k, b] = res[0:128] + res[128:256] + res[256:384]
            return carry
        lax.fori_loop(0, 4, combine, 0)
        for cp in stage1(k):
            cp.start()
        if k >= 1:
            run_stage2(k - 1)
        if k >= 2:
            run_final(k - 2)
    run_stage2(CHUNKS - 1)
    run_final(CHUNKS - 2)
    run_final(CHUNKS - 1)
    for k in range(CHUNKS):
        run_forward(k)
    for k in range(CHUNKS):
        sib = o_part(cx, 1 - core, k)
        rdma(sib, sib, os_s.at[k], os_r.at[k], sibling).wait_recv()
        store_out(cx, 1 - core, k, 2).start()
    for k in range(CHUNKS):
        far = o_part(1 - cx, 1 - core, k)
        rdma(far, far, of_s.at[k], of_r.at[k], sibling).wait_recv()
        store_out(1 - cx, 1 - core, k, 3).start()

    ctx_cp.wait_send()
    m_cp.wait_send()
    ish_cp.wait_send()
    for cp in u_cps:
        cp.wait_send()
    for cp in fwd:
        cp.wait_send()
    for e in range(EXPERTS):
        rdma(in_part(e, core), in_part(e, core), in_s.at[e], in_r.at[e], sibling).wait_send()
    for k in range(CHUNKS):
        for cp in stage1(k):
            cp.wait_send()
        stage2(k).wait_send()
        mine = o_part(cx, core, k)
        theirs = o_part(1 - cx, core, k)
        rdma(mine, mine, os_s.at[k], os_r.at[k], sibling).wait_send()
        rdma(mine, mine, ox_s.at[k], ox_r.at[k], x_nbr).wait_send()
        rdma(theirs, theirs, of_s.at[k], of_r.at[k], sibling).wait_send()
        store_out(cx, core, k, 0).wait()
        store_out(1 - cx, core, k, 1).wait()
        store_out(cx, 1 - core, k, 2).wait()
        store_out(1 - cx, 1 - core, k, 3).wait()


def moe(ctx, routes, gain, hidden, w_o, sg, su, sd, wg, wu, wd):
    any_spec = pl.BlockSpec(memory_space=pl.ANY)
    vmem_spec = pl.BlockSpec(memory_space=pltpu.VMEM)
    dma = pltpu.SemaphoreType.DMA
    return pl.pallas_call(
        moe_kernel,
        out_shape=jax.ShapeDtypeStruct(hidden.shape, BF16),
        in_specs=[vmem_spec] * 3 + [any_spec] * 8,
        out_specs=any_spec,
        scratch_shapes=[
            pltpu.VMEM((RING, DIM, 512), BF16),
            pltpu.VMEM((ROWS, HALF), BF16),
            pltpu.VMEM((ROWS, HALF), BF16),
            pltpu.VMEM((2, ROWS, HALF), BF16),
            pltpu.VMEM((4, ROWS, DIM), BF16),
            pltpu.VMEM((2, ROWS, 512), BF16),
            pltpu.VMEM((ROWS, HALF), F32),
            pltpu.VMEM((2, 16, 2 * ROWS), F32),
            pltpu.VMEM((4, EXPERTS * SLOTS, ROWS), BF16),
            pltpu.VMEM((4, 3 * ROWS, EXPERTS * SLOTS), BF16),
            pltpu.VMEM((EXPERTS, 4 * SLOTS, DIM), BF16),
            pltpu.VMEM((EXPERTS, 4 * SLOTS, 1024), BF16),
            pltpu.VMEM((4, EXPERTS * SLOTS, CW), BF16),
            pltpu.VMEM((CHUNKS, 4, ROWS, CW), F32),
            pltpu.VMEM((CHUNKS, 2, ROWS, CW), F32),
            pltpu.VMEM((CHUNKS, ROWS, CW), F32),
            pltpu.VMEM((CHUNKS, ROWS, CW), F32),
            pltpu.VMEM((2, 2, CHUNKS, ROWS, CW), BF16),
            dma((RING,)), dma, dma((4,)), dma((4,)),
            dma((3,)), dma((3,)), dma((3,)), dma((3,)),
            dma((EXPERTS,)), dma((EXPERTS,)),
            dma((CHUNKS, 2)), dma((CHUNKS, 2)), dma((CHUNKS,)), dma((CHUNKS,)),
            dma((CHUNKS,)), dma((CHUNKS,)), dma((CHUNKS,)), dma((CHUNKS,)), dma((CHUNKS,)), dma((CHUNKS,)),
            dma((4, CHUNKS)),
        ],
        compiler_params=pltpu.CompilerParams(vmem_limit_bytes=62 * 1024 * 1024, collective_id=0, has_side_effects=True),
        name='experts',
    )(ctx, routes, gain, hidden, w_o, sg, su, sd, wg, wu, wd)


def solution(mesh):
    batch_spec = P(('inst', 'dev'))
    layer_batch = P(None, ('inst', 'dev'))
    expert_spec = P(None, 'dev')

    def device_fn(hidden, k_cache, v_cache, cache_lens, expert_ids, route_gates, attn_gain, ffn_gain, w_q, w_kv, w_o, shared_gate, shared_up, shared_down, w_gate, w_up, w_down):
        routes = jnp.concatenate([expert_ids[0].astype(F32).T, route_gates[0].T], axis=0)
        ctx = attention(hidden, cache_lens, attn_gain, w_q, w_kv, k_cache, v_cache)
        return moe(ctx, routes, ffn_gain, hidden, w_o, shared_gate, shared_up, shared_down, w_gate, w_up, w_down)

    in_specs = (batch_spec, layer_batch, layer_batch, batch_spec, layer_batch, layer_batch, P(), P(), P(), P(), P(), P(), P(), P(), expert_spec, expert_spec, expert_spec)
    return jax.shard_map(device_fn, mesh=mesh, in_specs=in_specs, out_specs=batch_spec, check_vma=False)
```

time: 945 us -> 122 us (0.13)
  waiting for transfers between devices: 598 us -> 0 us
  Pallas kernels: 0 us -> 118 us
  blocking collectives: 95.7 us -> 0 us
  matrix products: 87.6 us -> 0 us
  local copies, waits for them, and re-layouts: 88 us -> 2.3 us
  other arithmetic: 41.6 us -> 1.99 us
  between operations: 13.8 us -> 0.02 us
  starting transfers between devices: 13 us -> 0 us
    ppermute x2 -> x0, waiting for transfers between devices: 492 us -> none  [the longest x1 321 us: device_fn(): back_buf = lax.ppermute(expert_res, 'side', to_attn)]
    pallas_call x0 -> x2, Pallas kernels: none -> 118 us  [the longest x1 85.1 us: moe(): pl.pallas_call(moe_kernel, out_shape=jax.ShapeDtypeStruct(hidden.shape, B...]
    all_to_all x1 -> x0, blocking collectives: 95.7 us -> none  [device_fn(): lax.all_to_all(send_buf.reshape(num_dev, local_experts, capacity, model_d...]
    dot_general x9 -> x0, matrix products: 87.6 us -> none  [the longest x1 40 us: attend(): jnp.einsum('tkgd,tksd->tkgs', q_rows, key_cache, preferred_element_type=j...]
    all_to_all x1 -> x0, waiting for transfers between devices: 87.6 us -> none  [device_fn(): lax.all_to_all(back_buf, 'dev', 0, 0)]
    gather x3 -> x0, local copies, waits for them, and re-layouts: 33.8 us -> none  [the longest x2 20.6 us: gather_rows(): picked = jnp.take(in_rows, owner_idx.astype(jnp.int32), axis=0)]
    another operation x4 -> x0, other arithmetic: 19.8 us -> none
    all_gather x1 -> x0, waiting for transfers between devices: 18.3 us -> none  [device_fn(): gathered = lax.all_gather(x_state, 'side')]
  transfers between devices with their start and end apart: 4 -> 0, of which waited for: 4 -> 0; matrix products, arithmetic and copies ran while one was open for 0% -> 0% of each run, Pallas kernels for 0% -> 0%
where the time goes in v1:
time: 122 us
  Pallas kernels  118 us (97%)
  local copies, waits for them, and re-layouts  2.3 us (2%)
  other arithmetic  1.99 us (2%)
    pallas_call x1, Pallas kernels, moe(): pl.pallas_call(moe_kernel, out_shape=jax.ShapeDtypeStruct(hidden.shape, B...  85.1 us
    pallas_call x1, Pallas kernels, attention(): pl.pallas_call(attn_kernel, out_shape=jax.ShapeDtypeStruct((ROWS, HALF),...  32.7 us

profile of v1, /device:TPU:0, one launch (start us, length us, event | category | flops | bytes accessed | tf_op | source)
XLA Modules:
  0.0 122.1 jit_solution(18211462996988288794)
XLA Ops:
  0.0 0.7 convert_bitcast_fusion
  0.7 1.3 %pad_maximum_fusion.rt_ref = f32[16,256]{1,0:T(8,128)} fusion(f32[8,256]{1,0:T(8,128)} %bitcast.7, f32[8,256]{1,0:T(8,128)S(1)} %convert_bitcast_fusion), kind=kLoop, calls=%fused_computation | loop fusion | flops 4096 | bytes 32768 | tf_op jit(solution)/shard_map/concatenate | solution.py:557
  2.0 32.7 %attend.1.ctx_ref = bf16[128,1024]{1,0:T(8,128)(2,1)} custom-call(s32[256]{0:T(256)} %lens_ref.1, bf16[256,2048]{1,0:T(8,128)(2,1)} %hidden_ref.3, f32[1,2048]{1,0:T(1,128)} %gain_ref.2, f32[1,128]{1,0:T(1,128)} %constant.2.clone.freq_ref, bf16[1,2048,2048]{2,1,0:T(8,128)(2,1)} %wq_ref.1, bf16[1,2048,4096]{2,1,0:T(8,128)(2,1)} %wkv_ref.1, ...), custom_call_target="tpu_custom_call" | custom-call | tf_op jit(solution)/shard_map/attend/pallas_call | solution.py:171
  34.7 85.1 %experts.1 = bf16[256,2048]{1,0:T(8,128)(2,1)} custom-call(bf16[128,1024]{1,0:T(8,128)(2,1)} %attend.1.ctx_ref, f32[16,256]{1,0:T(8,128)} %pad_maximum_fusion.rt_ref, f32[1,2048]{1,0:T(1,128)} %gain_ref.3, bf16[256,2048]{1,0:T(8,128)(2,1)} %hidden_ref.3, bf16[1,2048,2048]{2,1,0:T(8,128)(2,1)} %wo_ref.1, bf16[1,2048,1024]{2,1,0:T(8,128)(2,1)} %sg_ref.1, ...), custom_call_target="tpu_custom_call" | custom-call | tf_op jit(solution)/shard_map/experts/pallas_call | solution.py:515
  119.8 2.3 %copy.20 = bf16[256,2048]{1,0:T(8,128)(2,1)} copy(bf16[256,2048]{1,0:T(8,128)(2,1)} %experts.1) | data formatting | bytes 2097152

commit v2 on v1

v2 whole, which is shorter than its diff:
```python
import functools

import numpy as np
import jax
import jax.numpy as jnp
from jax import lax
from jax.experimental import pallas as pl
from jax.experimental.pallas import tpu as pltpu
from jax.sharding import PartitionSpec as P

NORM_EPS = 1e-6
ROPE_BASE = 10000.0
MESH = pl.DeviceIdType.MESH
LAST_DIMS = (((1,), (1,)), ((), ()))
F32 = jnp.float32
BF16 = jnp.bfloat16

ROWS = 128
HEADS = 8
HD = 128
DIM = 2048
HALF = DIM // 2
GROUP = 8
KV_RING = 8
RING = 16
QW = 512
LAYER = 0
S_CTX, S_IDS, S_M, S_IN, S_GATES = range(5)
X_LINK, Y_LINK, RELAY = range(3)
EXPERTS = 16
SLOTS = 32
CHUNKS = 4
CW = HALF // CHUNKS
ROWS_Y = 96


def norm_rows(rows_f, gain):
    inv_rms = lax.rsqrt(jnp.mean(rows_f * rows_f, axis=-1, keepdims=True) + NORM_EPS)
    return (rows_f * inv_rms * gain).astype(BF16)


def attn_kernel(lens_ref, hidden_ref, gain_ref, freq_ref, wq_ref, wkv_ref, kc_ref, vc_ref, ctx_ref,
                xbuf, wbuf, pos_buf, qbuf, nkbuf, nvbuf, cbuf, sbuf, pbuf, kbuf, vbuf, xsem, wsem, ksem, vsem):
    side = lax.axis_index('side')
    row0 = (side // 2) * ROWS
    core = side % 2
    h0 = core * HEADS
    groups = ROWS // GROUP

    def size_of(tok):
        return (lens_ref[row0 + tok] + 15) & -16

    def v_size_of(tok):
        return jnp.where(tok < KV_RING * GROUP, HD, size_of(tok))

    def start_group(grp):
        slot = grp & (KV_RING - 1)
        for i in range(GROUP):
            tok = grp * GROUP + i
            for src, dst, sem, size in ((kc_ref, kbuf, ksem, size_of), (vc_ref, vbuf, vsem, v_size_of)):
                size = pl.multiple_of(size(tok), 16)
                pltpu.make_async_copy(src.at[LAYER, row0 + tok, pl.ds(h0, HEADS), pl.ds(0, size), :],
                                      dst.at[slot, :, pl.ds(i * HD, size), :], sem.at[slot]).start()

    def wait_group(grp, buf, sem):
        slot = grp & (KV_RING - 1)
        size = size_of if buf is kbuf else v_size_of
        total = sum(size(grp * GROUP + i) for i in range(GROUP))
        whole = buf.at[slot, :, pl.ds(0, pl.multiple_of(total, 16)), :]
        pltpu.make_async_copy(whole, whole, sem.at[slot]).wait()

    x_cp = pltpu.make_async_copy(hidden_ref.at[pl.ds(row0, ROWS), :], xbuf, xsem)
    x_cp.start()
    w_cps = []
    for i in range(6):
        kind, j = i // 2, i % 2
        col = core * HALF + j * QW
        if kind == 0:
            src = wq_ref.at[LAYER, :, pl.ds(col, QW)]
        else:
            src = wkv_ref.at[LAYER, :, pl.ds((kind - 1) * DIM + col, QW)]
        cp = pltpu.make_async_copy(src, wbuf.at[i], wsem.at[i])
        cp.start()
        w_cps.append(cp)

    def fill_pos(i, carry):
        for r in range(8):
            row = i * 8 + r
            pos_buf[pl.ds(row, 1), :] = jnp.full((1, HD), lens_ref[row0 + row].astype(F32), F32)
        return carry
    lax.fori_loop(0, ROWS // 8, fill_pos, 0)
    angles = pos_buf[...] * freq_ref[...]
    cosine = jnp.cos(angles)
    lane = lax.broadcasted_iota(jnp.int32, (ROWS, HD), 1)
    sine = jnp.sin(angles)
    sine = jnp.where(lane < HD // 2, -sine, sine)

    x_cp.wait()
    normed = norm_rows(xbuf[...].astype(F32), gain_ref[...])
    lax.fori_loop(0, 3, lambda g, c: (start_group(g), c)[1], 0)
    for i in range(6):
        kind, j = i // 2, i % 2
        w_cps[i].wait()
        res = jnp.dot(normed, wbuf[i], preferred_element_type=F32).astype(BF16).astype(F32)
        for hh in range(4):
            h = j * 4 + hh
            val = res[:, hh * HD:(hh + 1) * HD]
            if kind < 2:
                val = (val * cosine + pltpu.roll(val, HD // 2, 1) * sine).astype(BF16).astype(F32)
            (qbuf, nkbuf, nvbuf)[kind][:, h * HD:(h + 1) * HD] = val
        if i == 1:
            lax.fori_loop(3, KV_RING, lambda g, c: (start_group(g), c)[1], 0)

    row_id = lax.broadcasted_iota(jnp.int32, (2 * GROUP, HD), 0) & (GROUP - 1)
    lane_f = lax.broadcasted_iota(jnp.int32, (GROUP, HD), 1).astype(F32)

    def rows_of(grp):
        return pl.ds(pl.multiple_of(grp * GROUP, GROUP), GROUP)

    def pair_of(ref, rows, hp):
        return jnp.concatenate([ref[rows, (2 * hp + p) * HD:(2 * hp + p + 1) * HD] for p in range(2)], axis=0)

    def score_group(grp):
        slot = grp & (KV_RING - 1)
        rows = rows_of(grp)
        valid = lane_f < pos_buf[rows, :]
        valid = jnp.concatenate([valid, valid], axis=0)
        for hp in range(HEADS // 2):
            zero = jnp.zeros((GROUP, HD), F32)
            first = jnp.concatenate([qbuf[rows, 2 * hp * HD:(2 * hp + 1) * HD], zero], axis=0)
            second = jnp.concatenate([zero, qbuf[rows, (2 * hp + 1) * HD:(2 * hp + 2) * HD]], axis=0)
            lhs = jnp.concatenate([first, second], axis=1).astype(BF16)
            rhs = jnp.concatenate([kbuf[slot, 2 * hp], kbuf[slot, 2 * hp + 1]], axis=1)
            full = lax.dot_general(lhs, rhs, LAST_DIMS, preferred_element_type=F32)
            sc = full[:, 0:HD]
            for i in range(1, GROUP):
                sc = jnp.where(row_id == i, full[:, i * HD:(i + 1) * HD], sc)
            sbuf[grp & 1, hp] = jnp.where(valid, sc * (HD ** -0.5), -jnp.inf)

    def soften_group(grp):
        rows = rows_of(grp)
        for hp in range(HEADS // 2):
            sc = sbuf[grp & 1, hp]
            self_sc = jnp.sum(pair_of(qbuf, rows, hp) * pair_of(nkbuf, rows, hp), axis=-1, keepdims=True) * (HD ** -0.5)
            peak = jnp.maximum(jnp.max(sc, axis=-1, keepdims=True), self_sc)
            wts = jnp.exp(sc - peak)
            self_w = jnp.exp(self_sc - peak)
            denom = jnp.sum(wts, axis=-1, keepdims=True) + self_w
            prob = wts / denom
            self_p = (self_w / denom).astype(BF16).astype(F32)
            wide = jnp.concatenate([jnp.where(row_id == i, prob, 0.0) for i in range(GROUP)], axis=1).astype(BF16)
            pbuf[grp & 1, hp] = wide
            for p in range(2):
                cols = slice((2 * hp + p) * HD, (2 * hp + p + 1) * HD)
                cbuf[rows, cols] = self_p[p * GROUP:(p + 1) * GROUP] * nvbuf[rows, cols]

    def value_group(grp):
        slot = grp & (KV_RING - 1)
        rows = rows_of(grp)
        for hp in range(HEADS // 2):
            rhs = jnp.concatenate([vbuf[slot, 2 * hp], vbuf[slot, 2 * hp + 1]], axis=1)
            ctx = jnp.dot(pbuf[grp & 1, hp], rhs, preferred_element_type=F32)
            for p in range(2):
                cols = slice((2 * hp + p) * HD, (2 * hp + p + 1) * HD)
                cbuf[rows, cols] += ctx[p * GROUP:(p + 1) * GROUP, p * HD:(p + 1) * HD]

    last = groups - 1
    wait_group(jnp.int32(0), kbuf, ksem)
    score_group(jnp.int32(0))
    wait_group(jnp.int32(1), kbuf, ksem)
    soften_group(jnp.int32(0))
    score_group(jnp.int32(1))

    def body(grp, carry):
        wait_group(grp - 1, vbuf, vsem)
        wait_group(grp + 1, kbuf, ksem)
        value_group(grp - 1)
        soften_group(grp)
        score_group(grp + 1)

        @pl.when(grp - 1 + KV_RING < groups)
        def _():
            start_group(grp - 1 + KV_RING)
        return carry
    lax.fori_loop(1, last, body, 0)
    wait_group(jnp.int32(last - 1), vbuf, vsem)
    wait_group(jnp.int32(last), vbuf, vsem)
    value_group(jnp.int32(last - 1))
    soften_group(jnp.int32(last))
    value_group(jnp.int32(last))
    ctx_ref[...] = cbuf[...].astype(BF16)


def attention(hidden, lens, gain, w_q, w_kv, k_cache, v_cache):
    freq = ROPE_BASE ** (-np.arange(HD // 2, dtype=np.float64) * 2.0 / HD)
    freq = np.concatenate([freq, freq])[None, :].astype(np.float32)
    any_spec = pl.BlockSpec(memory_space=pl.ANY)
    vmem_spec = pl.BlockSpec(memory_space=pltpu.VMEM)
    return pl.pallas_call(
        attn_kernel,
        out_shape=jax.ShapeDtypeStruct((ROWS, HALF), BF16),
        in_specs=[pl.BlockSpec(memory_space=pltpu.SMEM), any_spec, vmem_spec, vmem_spec] + [any_spec] * 4,
        out_specs=vmem_spec,
        scratch_shapes=[
            pltpu.VMEM((ROWS, DIM), BF16),
            pltpu.VMEM((6, DIM, QW), BF16),
            pltpu.VMEM((ROWS, HD), F32),
            pltpu.VMEM((ROWS, HALF), F32),
            pltpu.VMEM((ROWS, HALF), F32),
            pltpu.VMEM((ROWS, HALF), F32),
            pltpu.VMEM((ROWS, HALF), F32),
            pltpu.VMEM((2, HEADS // 2, 2 * GROUP, HD), F32),
            pltpu.VMEM((2, HEADS // 2, 2 * GROUP, GROUP * HD), BF16),
            pltpu.VMEM((KV_RING, HEADS, GROUP * HD, HD), BF16),
            pltpu.VMEM((KV_RING, HEADS, GROUP * HD, HD), BF16),
            pltpu.SemaphoreType.DMA,
            pltpu.SemaphoreType.DMA((6,)),
            pltpu.SemaphoreType.DMA((KV_RING,)),
            pltpu.SemaphoreType.DMA((KV_RING,)),
        ],
        compiler_params=pltpu.CompilerParams(vmem_limit_bytes=60 * HALF * HALF),
        name='attend',
    )(lens, hidden, gain, jnp.asarray(freq), w_q, w_kv, k_cache, v_cache)


def moe_kernel(gain_ref, ctx_ref, ids_ref, gates_ref, hidden_ref, wo_ref, sg_ref, su_ref, sd_ref, wg_ref, wu_ref, wd_ref, out_ref,
               ring, ctx_own, ctx_sib, xbuf, mbuf, uall, ish, base, ids_all, gates_all, dmat, cg, xe, inner, ybuf, pbuf,
               recv1, send2, recv2, oall,
               ring_sem, x_sem, misc_s, misc_r, u_s, u_r, uf_s, uf_r, in_s, in_r, p1_s, p1_r, p2_s, p2_r,
               os_s, os_r, ox_s, ox_r, of_s, of_r, out_sem):
    inst = lax.axis_index('inst')
    dy = lax.axis_index('dev')
    side = lax.axis_index('side')
    cx = side // 2
    core = side % 2
    blk0 = dy * 2 + cx
    col0 = core * HALF

    def dev_of(y, x, c):
        return (inst, y, x * 2 + c)
    sibling = dev_of(dy, cx, 1 - core)
    x_nbr = dev_of(dy, 1 - cx, core)
    y_nbr = dev_of(1 - dy, cx, core)

    def rdma(src, dst, s_sem, r_sem, dev):
        return pltpu.make_async_remote_copy(src_ref=src, dst_ref=dst, send_sem=s_sem, recv_sem=r_sem,
                                            device_id=dev, device_id_type=MESH)

    def start_wo(j):
        pltpu.make_async_copy(wo_ref.at[LAYER, :, pl.ds(col0 + j * QW, QW)], ring.at[j], ring_sem.at[j]).start()

    def start_gate(e, slot):
        pltpu.make_async_copy(wg_ref.at[LAYER, cx * EXPERTS + e, :, pl.ds(core * QW, QW)], ring.at[slot], ring_sem.at[slot]).start()

    def start_up(e, slot):
        pltpu.make_async_copy(wu_ref.at[LAYER, cx * EXPERTS + e, :, pl.ds(core * QW, QW)], ring.at[slot], ring_sem.at[slot]).start()

    def start_down(m, slot):
        k = m >> 2
        g = m & 3
        for i in range(4):
            pltpu.make_async_copy(wd_ref.at[LAYER, cx * EXPERTS + g * 4 + i, :, pl.ds(col0 + k * CW, CW)],
                                  ring.at[slot, pl.ds((i // 2) * HALF, HALF), pl.ds((i % 2) * CW, CW)],
                                  ring_sem.at[slot]).start()

    def wait_slot(slot):
        pltpu.make_async_copy(wg_ref.at[LAYER, 0, :, pl.ds(0, QW)], ring.at[slot], ring_sem.at[slot]).wait()

    def start_gu_block(b):
        e, up = (b - 5) // 2, (b - 5) % 2
        (start_up if up else start_gate)(e, b % RING)

    ctx_in = pltpu.make_async_copy(ctx_ref, ctx_own, x_sem.at[0])
    ctx_in.start()
    start_wo(0)
    start_wo(1)
    x_cp = pltpu.make_async_copy(hidden_ref.at[pl.ds(cx * ROWS, ROWS), pl.ds(col0, HALF)], xbuf, x_sem.at[1])
    x_cp.start()

    barrier = pltpu.get_barrier_semaphore()
    for dev in (sibling, x_nbr, y_nbr):
        pl.semaphore_signal(barrier, inc=1, device_id=dev, device_id_type=MESH)
    pltpu.make_async_copy(sg_ref.at[LAYER, :, pl.ds(core * QW, QW)], ring.at[2], ring_sem.at[2]).start()
    pltpu.make_async_copy(su_ref.at[LAYER, :, pl.ds(core * QW, QW)], ring.at[3], ring_sem.at[3]).start()
    ids_in = pltpu.make_async_copy(ids_ref, ids_all.at[dy], x_sem.at[2])
    gates_in = pltpu.make_async_copy(gates_ref, gates_all.at[dy], x_sem.at[3])
    ids_in.start()
    gates_in.start()
    pl.semaphore_wait(barrier, 3)

    ctx_in.wait()
    ctx_cp = rdma(ctx_own, ctx_sib, misc_s.at[S_CTX], misc_r.at[S_CTX], sibling)
    ctx_cp.start()

    own_row = core * HALF
    sib_row = (1 - core) * HALF
    wait_slot(0)
    wait_slot(1)
    for j in range(2):
        pltpu.make_async_copy(sd_ref.at[LAYER, :, pl.ds(col0 + j * QW, QW)], ring.at[4, pl.ds(j * HALF, HALF), :],
                              ring_sem.at[4]).start()
    for b in range(5, 9):
        start_gu_block(b)
    x_cp.wait()
    ctx_val = ctx_own[...]
    accs = [jnp.dot(ctx_val, ring[j, pl.ds(own_row, HALF), :], preferred_element_type=F32) for j in range(2)]
    ctx_cp.wait_recv()
    ctx_val = ctx_sib[...]
    for j in range(2):
        acc = accs[j] + jnp.dot(ctx_val, ring[j, pl.ds(sib_row, HALF), :], preferred_element_type=F32)
        mbuf[core, :, j * QW:(j + 1) * QW] = (xbuf[:, j * QW:(j + 1) * QW].astype(F32) + acc).astype(BF16)
    m_cp = rdma(mbuf.at[core], mbuf.at[core], misc_s.at[S_M], misc_r.at[S_M], sibling)
    m_cp.start()
    for b in range(9, 18):
        start_gu_block(b)
    m_other = rdma(mbuf.at[1 - core], mbuf.at[1 - core], misc_s.at[S_M], misc_r.at[S_M], sibling)
    m_other.wait_recv()
    m_lo = mbuf[0].astype(F32)
    m_hi = mbuf[1].astype(F32)
    total = jnp.sum(m_lo * m_lo, axis=-1, keepdims=True) + jnp.sum(m_hi * m_hi, axis=-1, keepdims=True)
    inv_rms = lax.rsqrt(total / DIM + NORM_EPS)
    uall[blk0, :, 0:HALF] = (m_lo * inv_rms * gain_ref[:, 0:HALF]).astype(BF16)
    uall[blk0, :, HALF:DIM] = (m_hi * inv_rms * gain_ref[:, HALF:DIM]).astype(BF16)

    blk_x = dy * 2 + 1 - cx
    blk_y = (1 - dy) * 2 + cx
    blk_d = (1 - dy) * 2 + 1 - cx

    def u_part(b, c, h):
        return uall.at[b, pl.ds(c * 64 + h * 32, 32), :]

    def u_copy(b, h, which, dev):
        return rdma(u_part(b, core, h), u_part(b, core, h), u_s.at[which, h], u_r.at[which, h], dev)

    def u_fwd(b, c, which, h):
        return rdma(u_part(b, c, h), u_part(b, c, h), uf_s.at[which, h], uf_r.at[which, h], sibling)
    u_copy(blk0, 0, X_LINK, x_nbr).start()
    u_copy(blk0, 1, Y_LINK, y_nbr).start()
    u_copy(blk0, 1, X_LINK, x_nbr).start()
    u_copy(blk0, 0, Y_LINK, y_nbr).start()
    ids_in.wait()
    gates_in.wait()
    ids_cp = rdma(ids_all.at[dy], ids_all.at[dy], misc_s.at[S_IDS], misc_r.at[S_IDS], y_nbr)
    gates_cp = rdma(gates_all.at[dy], gates_all.at[dy], misc_s.at[S_GATES], misc_r.at[S_GATES], y_nbr)
    ids_cp.start()
    gates_cp.start()

    wait_slot(2)
    wait_slot(3)
    u_own = uall[blk0]
    gate = jnp.dot(u_own, ring[2], preferred_element_type=F32)
    up = jnp.dot(u_own, ring[3], preferred_element_type=F32)
    ish[core] = (jax.nn.silu(gate) * up).astype(BF16)
    ish_cp = rdma(ish.at[core], ish.at[core], misc_s.at[S_IN], misc_r.at[S_IN], sibling)
    ish_cp.start()
    start_gu_block(18)
    start_gu_block(19)

    expert_id = dy * 32 + cx * EXPERTS + lax.broadcasted_iota(jnp.int32, (EXPERTS, ROWS), 0)
    before = (lax.broadcasted_iota(jnp.int32, (ROWS, ROWS), 0) < lax.broadcasted_iota(jnp.int32, (ROWS, ROWS), 1))
    before = jnp.where(before, 1.0, 0.0).astype(BF16)
    slot_id = lax.broadcasted_iota(jnp.int32, (SLOTS, ROWS), 0).astype(F32)

    def route_block(yb, xb):
        b = yb * 2 + xb
        hit = jnp.zeros((EXPERTS, ROWS), F32)
        wts = jnp.zeros((EXPERTS, ROWS), F32)
        for j in range(8):
            same = ids_all[yb, j:j + 1, xb * ROWS:(xb + 1) * ROWS] == expert_id
            hit = jnp.where(same, 1.0, hit)
            wts = jnp.where(same, gates_all[yb, j:j + 1, xb * ROWS:(xb + 1) * ROWS], wts)
        place = jnp.dot(hit.astype(BF16), before, preferred_element_type=F32)
        place = jnp.where(hit > 0.5, place, -1.0)
        pieces = []
        for e in range(EXPERTS):
            match = place[e:e + 1, :] == slot_id
            dmat[b, e * SLOTS:(e + 1) * SLOTS, :] = jnp.where(match, 1.0, 0.0).astype(BF16)
            pieces.append(jnp.where(match, wts[e:e + 1, :], 0.0))
        for q in range(4):
            part = jnp.concatenate(pieces[q * 4:(q + 1) * 4], axis=0).T
            high = part.astype(BF16)
            rest = part - high.astype(F32)
            mid = rest.astype(BF16)
            low = (rest - mid.astype(F32)).astype(BF16)
            cg[b, 0:ROWS, q * ROWS:(q + 1) * ROWS] = high
            cg[b, ROWS:256, q * ROWS:(q + 1) * ROWS] = mid
            cg[b, 256:384, q * ROWS:(q + 1) * ROWS] = low

    for xb in range(2):
        route_block(dy, xb)

    def dispatch(b):
        def one(n, carry):
            cols = pl.ds(pl.multiple_of(n * QW, QW), QW)
            rows = jnp.dot(dmat[b], uall[b, :, cols], preferred_element_type=F32).astype(BF16)
            for e in range(EXPERTS):
                xe[e, pl.ds(pl.multiple_of(b * SLOTS, SLOTS), SLOTS), cols] = rows[e * SLOTS:(e + 1) * SLOTS, :]
            return carry
        lax.fori_loop(0, DIM // QW, one, 0)

    u_copy(blk_x, 0, X_LINK, x_nbr).wait_recv()
    u_copy(blk_x, 0, RELAY, y_nbr).start()
    u_fwd(blk_x, core, X_LINK, 0).start()
    u_copy(blk_y, 1, Y_LINK, y_nbr).wait_recv()
    u_copy(blk_y, 1, RELAY, x_nbr).start()
    u_fwd(blk_y, core, Y_LINK, 1).start()

    rdma(ish.at[1 - core], ish.at[1 - core], misc_s.at[S_IN], misc_r.at[S_IN], sibling).wait_recv()
    wait_slot(4)
    for j in range(2):
        acc = jnp.dot(ish[0], ring[4, j * HALF:j * HALF + QW, :], preferred_element_type=F32)
        acc = acc + jnp.dot(ish[1], ring[4, j * HALF + QW:(j + 1) * HALF, :], preferred_element_type=F32)
        base[:, j * QW:(j + 1) * QW] = mbuf[core, :, j * QW:(j + 1) * QW].astype(F32) + acc.astype(BF16).astype(F32)
    start_gu_block(20)
    dispatch(blk0)
    rdma(ids_all.at[1 - dy], ids_all.at[1 - dy], misc_s.at[S_IDS], misc_r.at[S_IDS], y_nbr).wait_recv()
    rdma(gates_all.at[1 - dy], gates_all.at[1 - dy], misc_s.at[S_GATES], misc_r.at[S_GATES], y_nbr).wait_recv()
    u_copy(blk_x, 1, X_LINK, x_nbr).wait_recv()
    u_fwd(blk_x, core, X_LINK, 1).start()
    u_copy(blk_y, 0, Y_LINK, y_nbr).wait_recv()
    u_fwd(blk_y, core, Y_LINK, 0).start()
    for xb in range(2):
        route_block(1 - dy, xb)
    for h in range(2):
        u_fwd(blk_x, 1 - core, X_LINK, h).wait_recv()
    dispatch(blk_x)
    u_copy(blk_d, 0, RELAY, y_nbr).wait_recv()
    u_fwd(blk_d, core, RELAY, 0).start()
    u_copy(blk_d, 1, RELAY, x_nbr).wait_recv()
    u_fwd(blk_d, core, RELAY, 1).start()
    for h in range(2):
        u_fwd(blk_y, 1 - core, Y_LINK, h).wait_recv()
    dispatch(blk_y)
    for h in range(2):
        u_fwd(blk_d, 1 - core, RELAY, h).wait_recv()
    dispatch(blk_d)

    def in_part(e, c):
        return inner.at[e, :, pl.ds(pl.multiple_of(c * QW, QW), QW)]

    def in_copy(e, c):
        return rdma(in_part(e, c), in_part(e, c), in_s.at[e], in_r.at[e], sibling)

    def expert_pair(p, after):
        slots = [((5 + 4 * p + i) & (RING - 1)) for i in range(4)]
        for slot in slots:
            wait_slot(slot)
        for i in range(2):
            e = 2 * p + i
            rows = xe[e]
            gate = jnp.dot(rows, ring[slots[2 * i]], preferred_element_type=F32)
            up = jnp.dot(rows, ring[slots[2 * i + 1]], preferred_element_type=F32)
            inner[e, :, pl.ds(pl.multiple_of(core * QW, QW), QW)] = (jax.nn.silu(gate) * up).astype(BF16)
        for i in range(2):
            in_copy(2 * p + i, core).start()
        after(p, slots)

    def refill_experts(p, slots):
        for i in range(2):
            start_gate(2 * p + i + 8, slots[2 * i])
            start_up(2 * p + i + 8, slots[2 * i + 1])

    def refill_down(p, slots):
        for i in range(4):
            start_down(4 * (p - 4) + i, slots[i])

    lax.fori_loop(0, 4, lambda p, c: (expert_pair(p, refill_experts), c)[1], 0)
    lax.fori_loop(4, 8, lambda p, c: (expert_pair(p, refill_down), c)[1], 0)

    top = pl.ds(0, ROWS_Y)
    low = pl.ds(ROWS_Y, ROWS - ROWS_Y)

    def stage1(k, i):
        if i == 0:
            return [rdma(pbuf.at[k, blk_d, part, :], recv1.at[k, 0, part, :], p1_s.at[k, 0, a], p1_r.at[k, 0, a], dev)
                    for a, (part, dev) in enumerate(((top, y_nbr), (low, x_nbr)))]
        return [rdma(pbuf.at[k, b, part, :], recv1.at[k, 1, part, :], p1_s.at[k, 1, a], p1_r.at[k, 1, a], dev)
                for a, (b, part, dev) in enumerate(((blk_y, top, y_nbr), (blk_x, low, x_nbr)))]

    def stage2(k):
        return [rdma(send2.at[k, part, :], recv2.at[k, part, :], p2_s.at[k, a], p2_r.at[k, a], dev)
                for a, (part, dev) in enumerate(((top, x_nbr), (low, y_nbr)))]

    def run_stage2(k):
        first, second = stage1(k, 0)
        going = stage2(k)
        first.wait_recv()
        send2[k, 0:ROWS_Y, :] = pbuf[k, blk_x, 0:ROWS_Y, :] + recv1[k, 0, 0:ROWS_Y, :]
        going[0].start()
        second.wait_recv()
        send2[k, ROWS_Y:ROWS, :] = pbuf[k, blk_y, ROWS_Y:ROWS, :] + recv1[k, 0, ROWS_Y:ROWS, :]
        going[1].start()

    def o_part(x, c, k):
        return oall.at[x, c, k]

    def store_out(x, c, k, which):
        return pltpu.make_async_copy(o_part(x, c, k),
                                     out_ref.at[pl.ds(x * ROWS, ROWS), pl.ds(pl.multiple_of(c * HALF + k * CW, CW), CW)],
                                     out_sem.at[which, k])

    def o_sib(k, c):
        return rdma(o_part(cx, c, k), o_part(cx, c, k), os_s.at[k], os_r.at[k], sibling)

    def o_x(k, x):
        return rdma(o_part(x, core, k), o_part(x, core, k), ox_s.at[k], ox_r.at[k], x_nbr)

    def o_fwd(k, c):
        return rdma(o_part(1 - cx, c, k), o_part(1 - cx, c, k), of_s.at[k], of_r.at[k], sibling)

    def run_final(k):
        for cp in stage1(k, 1):
            cp.wait_recv()
        for cp in stage2(k):
            cp.wait_recv()
        routed = pbuf[k, blk0] + recv1[k, 1] + recv2[k]
        oall[cx, core, k] = (base[:, k * CW:(k + 1) * CW] + routed).astype(BF16)
        o_x(k, cx).start()
        o_sib(k, core).start()
        store_out(cx, core, k, 0).start()

    def run_forward(k):
        o_x(k, 1 - cx).wait_recv()
        o_fwd(k, core).start()
        store_out(1 - cx, core, k, 1).start()

    for e in range(EXPERTS):
        in_copy(e, 1 - core).wait_recv()

    for k in range(CHUNKS):
        def down_group(g, carry):
            slot = (5 + 4 * k + g) & (RING - 1)
            wait_slot(slot)
            for i in range(4):
                e = g * 4 + i
                w = ring[slot, (i // 2) * HALF:(i // 2 + 1) * HALF, (i % 2) * CW:(i % 2 + 1) * CW]
                res = jnp.dot(inner[e], w, preferred_element_type=F32).astype(BF16)
                for b in range(4):
                    ybuf[b, pl.ds(pl.multiple_of(e * SLOTS, SLOTS), SLOTS), :] = res[b * SLOTS:(b + 1) * SLOTS, :]
            return carry
        lax.fori_loop(0, 4, down_group, 0)

        def combine(b):
            res = jnp.dot(cg[b], ybuf[b], preferred_element_type=F32)
            pbuf[k, b] = res[0:ROWS] + res[ROWS:256] + res[256:384]
        combine(blk_d)
        for cp in stage1(k, 0):
            cp.start()
        combine(blk_y)
        combine(blk_x)
        for cp in stage1(k, 1):
            cp.start()
        combine(blk0)
        if k >= 1:
            run_stage2(k - 1)
        if k >= 2:
            run_final(k - 2)
    run_stage2(CHUNKS - 1)
    run_final(CHUNKS - 2)
    for k in range(CHUNKS - 1):
        run_forward(k)
    run_final(CHUNKS - 1)
    run_forward(CHUNKS - 1)
    for k in range(CHUNKS):
        o_sib(k, 1 - core).wait_recv()
        store_out(cx, 1 - core, k, 2).start()
    for k in range(CHUNKS):
        o_fwd(k, 1 - core).wait_recv()
        store_out(1 - cx, 1 - core, k, 3).start()

    for cp in (ctx_cp, m_cp, ids_cp, gates_cp, ish_cp):
        cp.wait_send()
    for h in range(2):
        u_copy(blk0, h, X_LINK, x_nbr).wait_send()
        u_copy(blk0, h, Y_LINK, y_nbr).wait_send()
        u_fwd(blk_x, core, X_LINK, h).wait_send()
        u_fwd(blk_y, core, Y_LINK, h).wait_send()
        u_fwd(blk_d, core, RELAY, h).wait_send()
    u_copy(blk_x, 0, RELAY, y_nbr).wait_send()
    u_copy(blk_y, 1, RELAY, x_nbr).wait_send()
    for e in range(EXPERTS):
        in_copy(e, core).wait_send()
    for k in range(CHUNKS):
        for cp in stage1(k, 0) + stage1(k, 1) + stage2(k):
            cp.wait_send()
        o_sib(k, core).wait_send()
        o_x(k, cx).wait_send()
        o_fwd(k, core).wait_send()
        store_out(cx, core, k, 0).wait()
        store_out(1 - cx, core, k, 1).wait()
        store_out(cx, 1 - core, k, 2).wait()
        store_out(1 - cx, 1 - core, k, 3).wait()


def moe(ctx, ids, gates, gain, hidden, w_o, sg, su, sd, wg, wu, wd):
    any_spec = pl.BlockSpec(memory_space=pl.ANY)
    vmem_spec = pl.BlockSpec(memory_space=pltpu.VMEM)
    dma = pltpu.SemaphoreType.DMA
    return pl.pallas_call(
        moe_kernel,
        out_shape=jax.ShapeDtypeStruct(hidden.shape, BF16),
        in_specs=[vmem_spec] + [any_spec] * 11,
        out_specs=any_spec,
        scratch_shapes=[
            pltpu.VMEM((RING, DIM, QW), BF16),
            pltpu.VMEM((ROWS, HALF), BF16),
            pltpu.VMEM((ROWS, HALF), BF16),
            pltpu.VMEM((ROWS, HALF), BF16),
            pltpu.VMEM((2, ROWS, HALF), BF16),
            pltpu.VMEM((4, ROWS, DIM), BF16),
            pltpu.VMEM((2, ROWS, QW), BF16),
            pltpu.VMEM((ROWS, HALF), F32),
            pltpu.VMEM((2, 8, 2 * ROWS), jnp.int32),
            pltpu.VMEM((2, 8, 2 * ROWS), F32),
            pltpu.VMEM((4, EXPERTS * SLOTS, ROWS), BF16),
            pltpu.VMEM((4, 3 * ROWS, EXPERTS * SLOTS), BF16),
            pltpu.VMEM((EXPERTS, 4 * SLOTS, DIM), BF16),
            pltpu.VMEM((EXPERTS, 4 * SLOTS, HALF), BF16),
            pltpu.VMEM((4, EXPERTS * SLOTS, CW), BF16),
            pltpu.VMEM((CHUNKS, 4, ROWS, CW), F32),
            pltpu.VMEM((CHUNKS, 2, ROWS, CW), F32),
            pltpu.VMEM((CHUNKS, ROWS, CW), F32),
            pltpu.VMEM((CHUNKS, ROWS, CW), F32),
            pltpu.VMEM((2, 2, CHUNKS, ROWS, CW), BF16),
            dma((RING,)), dma((4,)), dma((5,)), dma((5,)),
            dma((3, 2)), dma((3, 2)), dma((3, 2)), dma((3, 2)),
            dma((EXPERTS,)), dma((EXPERTS,)),
            dma((CHUNKS, 2, 2)), dma((CHUNKS, 2, 2)), dma((CHUNKS, 2)), dma((CHUNKS, 2)),
            dma((CHUNKS,)), dma((CHUNKS,)), dma((CHUNKS,)), dma((CHUNKS,)), dma((CHUNKS,)), dma((CHUNKS,)),
            dma((4, CHUNKS)),
        ],
        compiler_params=pltpu.CompilerParams(vmem_limit_bytes=60 * HALF * HALF, collective_id=0, has_side_effects=True),
        name='experts',
    )(gain, ctx, ids, gates, hidden, w_o, sg, su, sd, wg, wu, wd)


def solution(mesh):
    batch_spec = P(('inst', 'dev'))
    layer_batch = P(None, ('inst', 'dev'))
    expert_spec = P(None, 'dev')

    def device_fn(hidden, k_cache, v_cache, cache_lens, expert_ids, route_gates, attn_gain, ffn_gain, w_q, w_kv, w_o, shared_gate, shared_up, shared_down, w_gate, w_up, w_down):
        ctx = attention(hidden, cache_lens, attn_gain, w_q, w_kv, k_cache, v_cache)
        return moe(ctx, expert_ids[0].T, route_gates[0].T, ffn_gain, hidden, w_o, shared_gate, shared_up, shared_down, w_gate, w_up, w_down)

    in_specs = (batch_spec, layer_batch, layer_batch, batch_spec, layer_batch, layer_batch, P(), P(), P(), P(), P(), P(), P(), P(), expert_spec, expert_spec, expert_spec)
    return jax.shard_map(device_fn, mesh=mesh, in_specs=in_specs, out_specs=batch_spec, check_vma=False)
```

time: 122 us -> 96.5 us (0.79)
  Pallas kernels: 118 us -> 93.9 us
  other arithmetic: 1.99 us -> 0 us
    pallas_call x1, Pallas kernels: 85.1 us -> 68.4 us  [moe(): pl.pallas_call(moe_kernel, out_shape=jax.ShapeDtypeStruct(hidden.shape, B...]
    pallas_call x1, Pallas kernels: 32.7 us -> 25.4 us  [attention(): pl.pallas_call(attn_kernel, out_shape=jax.ShapeDtypeStruct((ROWS, HALF),...]
    concatenate x1 -> x0, other arithmetic: 1.3 us -> none  [device_fn(): jnp.concatenate([expert_ids[0].astype(F32).T, route_gates[0].T], axis=0)]
where the time goes in v2:
time: 96.5 us; the launch traced here: 96.2 us
  Pallas kernels  93.9 us (97%)
  local copies, waits for them, and re-layouts  2.3 us (2%)
    pallas_call x1, Pallas kernels, moe(): pl.pallas_call(moe_kernel, out_shape=jax.ShapeDtypeStruct(hidden.shape, B...  68.4 us
    pallas_call x1, Pallas kernels, attention(): pl.pallas_call(attn_kernel, out_shape=jax.ShapeDtypeStruct((ROWS, HALF),...  25.4 us
    unnamed x1, local copies, waits for them, and re-layouts  2.3 us

profile of v2, /device:TPU:0, one launch (start us, length us, event | category | flops | bytes accessed | tf_op | source)
XLA Modules:
  0.0 96.2 jit_solution(11680987873207723991)
XLA Ops:
  0.0 25.4 %attend.1.ctx_ref = bf16[128,1024]{1,0:T(8,128)(2,1)} custom-call(s32[256]{0:T(256)} %lens_ref.1, bf16[256,2048]{1,0:T(8,128)(2,1)} %hidden_ref.3, f32[1,2048]{1,0:T(1,128)} %gain_ref.2, f32[1,128]{1,0:T(1,128)} %constant.2.clone.freq_ref, bf16[1,2048,2048]{2,1,0:T(8,128)(2,1)} %wq_ref.1, bf16[1,2048,4096]{2,1,0:T(8,128)(2,1)} %wkv_ref.1, ...), custom_call_target="tpu_custom_call" | custom-call | tf_op jit(solution)/shard_map/attend/pallas_call | solution.py:199
  25.4 68.4 %experts.1 = bf16[256,2048]{1,0:T(8,128)(2,1)} custom-call(f32[1,2048]{1,0:T(1,128)} %gain_ref.3, bf16[128,1024]{1,0:T(8,128)(2,1)} %attend.1.ctx_ref, s32[8,256]{1,0:T(8,128)} %bitcast.6, f32[8,256]{1,0:T(8,128)} %bitcast.7, bf16[256,2048]{1,0:T(8,128)(2,1)} %hidden_ref.3, bf16[1,2048,2048]{2,1,0:T(8,128)(2,1)} %wo_ref.1, bf16[1,2048,1024]{2,1,0:T(8,128)(2,1)} %sg_ref.1, ...), custom_call_target="tpu_custom_call" | custom-call | tf_op jit(solution)/shard_map/experts/pallas_call | solution.py:599
  93.9 2.3 %copy.20 = bf16[256,2048]{1,0:T(8,128)(2,1)} copy(bf16[256,2048]{1,0:T(8,128)(2,1)} %experts.1) | data formatting | bytes 2097152

commit v3 on v2

--- a/solution.py
+++ b/solution.py
@@ -20,13 +20,16 @@
 HD = 128
 DIM = 2048
 HALF = DIM // 2
+HH = HEADS // 2
 GROUP = 8
 KV_RING = 8
-RING = 16
+PAIRS = ROWS // (2 * GROUP)
+RING = 20
 QW = 512
 LAYER = 0
 S_CTX, S_IDS, S_M, S_IN, S_GATES = range(5)
 X_LINK, Y_LINK, RELAY = range(3)
+XE = 8
 EXPERTS = 16
 SLOTS = 32
 CHUNKS = 4
@@ -40,48 +43,55 @@
 
 
 def attn_kernel(lens_ref, hidden_ref, gain_ref, freq_ref, wq_ref, wkv_ref, kc_ref, vc_ref, ctx_ref,
-                xbuf, wbuf, pos_buf, qbuf, nkbuf, nvbuf, cbuf, sbuf, pbuf, kbuf, vbuf, xsem, wsem, ksem, vsem):
+                xbuf, nbuf, cosbuf, sinbuf, wbuf, pos_buf, qbuf, nkbuf, nvbuf, cbuf, sbuf, pbuf, kbuf, vbuf, xsem, wsem, ksem, vsem):
     side = lax.axis_index('side')
     row0 = (side // 2) * ROWS
     core = side % 2
     h0 = core * HEADS
-    groups = ROWS // GROUP
-
-    def size_of(tok):
+
+    def size_of(unit, tok):
         return (lens_ref[row0 + tok] + 15) & -16
 
-    def v_size_of(tok):
-        return jnp.where(tok < KV_RING * GROUP, HD, size_of(tok))
-
-    def start_group(grp):
-        slot = grp & (KV_RING - 1)
-        for i in range(GROUP):
-            tok = grp * GROUP + i
-            for src, dst, sem, size in ((kc_ref, kbuf, ksem, size_of), (vc_ref, vbuf, vsem, v_size_of)):
-                size = pl.multiple_of(size(tok), 16)
-                pltpu.make_async_copy(src.at[LAYER, row0 + tok, pl.ds(h0, HEADS), pl.ds(0, size), :],
-                                      dst.at[slot, :, pl.ds(i * HD, size), :], sem.at[slot]).start()
-
-    def wait_group(grp, buf, sem):
-        slot = grp & (KV_RING - 1)
+    def v_size_of(unit, tok):
+        return jnp.where(unit < KV_RING, HD, size_of(unit, tok))
+
+    def first_token(unit, d):
+        return (unit & (PAIRS - 1)) * (2 * GROUP) + d * GROUP
+
+    def start_unit(unit):
+        slot = unit & (KV_RING - 1)
+        heads = pl.ds(h0 + (unit >> 3) * HH, HH)
+        for d in range(2):
+            for i in range(GROUP):
+                tok = first_token(unit, d) + i
+                for src, dst, sem, size in ((kc_ref, kbuf, ksem, size_of), (vc_ref, vbuf, vsem, v_size_of)):
+                    size = pl.multiple_of(size(unit, tok), 16)
+                    pltpu.make_async_copy(src.at[LAYER, row0 + tok, heads, pl.ds(0, size), :],
+                                          dst.at[slot, pl.ds(d * HH, HH), pl.ds(i * HD, size), :], sem.at[slot, d]).start()
+
+    def wait_unit(unit, buf, sem):
+        slot = unit & (KV_RING - 1)
         size = size_of if buf is kbuf else v_size_of
-        total = sum(size(grp * GROUP + i) for i in range(GROUP))
-        whole = buf.at[slot, :, pl.ds(0, pl.multiple_of(total, 16)), :]
-        pltpu.make_async_copy(whole, whole, sem.at[slot]).wait()
+        for d in range(2):
+            total = sum(size(unit, first_token(unit, d) + i) for i in range(GROUP))
+            whole = buf.at[slot, pl.ds(d * HH, HH), pl.ds(0, pl.multiple_of(total, 16)), :]
+            pltpu.make_async_copy(whole, whole, sem.at[slot, d]).wait()
 
     x_cp = pltpu.make_async_copy(hidden_ref.at[pl.ds(row0, ROWS), :], xbuf, xsem)
     x_cp.start()
-    w_cps = []
-    for i in range(6):
-        kind, j = i // 2, i % 2
+
+    def weight_copy(j, kind):
         col = core * HALF + j * QW
         if kind == 0:
             src = wq_ref.at[LAYER, :, pl.ds(col, QW)]
         else:
             src = wkv_ref.at[LAYER, :, pl.ds((kind - 1) * DIM + col, QW)]
-        cp = pltpu.make_async_copy(src, wbuf.at[i], wsem.at[i])
-        cp.start()
-        w_cps.append(cp)
+        return pltpu.make_async_copy(src, wbuf.at[j * 3 + kind], wsem.at[j * 3 + kind])
+
+    def start_units(lo, hi):
+        lax.fori_loop(lo, hi, lambda u, c: (start_unit(u), c)[1], 0)
+    for kind in range(3):
+        weight_copy(0, kind).start()
 
     def fill_pos(i, carry):
         for r in range(8):
@@ -95,53 +105,59 @@
     sine = jnp.sin(angles)
     sine = jnp.where(lane < HD // 2, -sine, sine)
 
+    start_units(0, 2)
+    for kind in range(3):
+        weight_copy(1, kind).start()
     x_cp.wait()
-    normed = norm_rows(xbuf[...].astype(F32), gain_ref[...])
-    lax.fori_loop(0, 3, lambda g, c: (start_group(g), c)[1], 0)
-    for i in range(6):
-        kind, j = i // 2, i % 2
-        w_cps[i].wait()
-        res = jnp.dot(normed, wbuf[i], preferred_element_type=F32).astype(BF16).astype(F32)
-        for hh in range(4):
-            h = j * 4 + hh
-            val = res[:, hh * HD:(hh + 1) * HD]
-            if kind < 2:
-                val = (val * cosine + pltpu.roll(val, HD // 2, 1) * sine).astype(BF16).astype(F32)
-            (qbuf, nkbuf, nvbuf)[kind][:, h * HD:(h + 1) * HD] = val
-        if i == 1:
-            lax.fori_loop(3, KV_RING, lambda g, c: (start_group(g), c)[1], 0)
+    nbuf[...] = norm_rows(xbuf[...].astype(F32), gain_ref[...])
+    cosbuf[...] = cosine
+    sinbuf[...] = sine
+    start_units(2, KV_RING)
+
+    def project(j):
+        for kind in range(3):
+            weight_copy(j, kind).wait()
+            res = jnp.dot(nbuf[...], wbuf[j * 3 + kind], preferred_element_type=F32).astype(BF16).astype(F32)
+            for hh in range(HH):
+                h = j * HH + hh
+                val = res[:, hh * HD:(hh + 1) * HD]
+                if kind < 2:
+                    val = (val * cosbuf[...] + pltpu.roll(val, HD // 2, 1) * sinbuf[...]).astype(BF16).astype(F32)
+                (qbuf, nkbuf, nvbuf)[kind][:, h * HD:(h + 1) * HD] = val
+    project(0)
 
     row_id = lax.broadcasted_iota(jnp.int32, (2 * GROUP, HD), 0) & (GROUP - 1)
     lane_f = lax.broadcasted_iota(jnp.int32, (GROUP, HD), 1).astype(F32)
 
-    def rows_of(grp):
-        return pl.ds(pl.multiple_of(grp * GROUP, GROUP), GROUP)
-
-    def pair_of(ref, rows, hp):
-        return jnp.concatenate([ref[rows, (2 * hp + p) * HD:(2 * hp + p + 1) * HD] for p in range(2)], axis=0)
-
-    def score_group(grp):
-        slot = grp & (KV_RING - 1)
-        rows = rows_of(grp)
-        valid = lane_f < pos_buf[rows, :]
-        valid = jnp.concatenate([valid, valid], axis=0)
-        for hp in range(HEADS // 2):
-            zero = jnp.zeros((GROUP, HD), F32)
-            first = jnp.concatenate([qbuf[rows, 2 * hp * HD:(2 * hp + 1) * HD], zero], axis=0)
-            second = jnp.concatenate([zero, qbuf[rows, (2 * hp + 1) * HD:(2 * hp + 2) * HD]], axis=0)
+    def parts_of(unit):
+        for d in range(2):
+            rows = pl.ds(pl.multiple_of(first_token(unit, d), GROUP), GROUP)
+            for hp in range(2):
+                head = (unit >> 3) * HH + 2 * hp
+                cols = [pl.ds(pl.multiple_of((head + p) * HD, HD), HD) for p in range(2)]
+                yield 2 * d + hp, d * HH + 2 * hp, rows, cols
+
+    def score_unit(unit):
+        slot = unit & (KV_RING - 1)
+        zero = jnp.zeros((GROUP, HD), F32)
+        for n, at, rows, cols in parts_of(unit):
+            valid = lane_f < pos_buf[rows, :]
+            valid = jnp.concatenate([valid, valid], axis=0)
+            first = jnp.concatenate([qbuf[rows, cols[0]], zero], axis=0)
+            second = jnp.concatenate([zero, qbuf[rows, cols[1]]], axis=0)
             lhs = jnp.concatenate([first, second], axis=1).astype(BF16)
-            rhs = jnp.concatenate([kbuf[slot, 2 * hp], kbuf[slot, 2 * hp + 1]], axis=1)
+            rhs = jnp.concatenate([kbuf[slot, at], kbuf[slot, at + 1]], axis=1)
             full = lax.dot_general(lhs, rhs, LAST_DIMS, preferred_element_type=F32)
             sc = full[:, 0:HD]
             for i in range(1, GROUP):
                 sc = jnp.where(row_id == i, full[:, i * HD:(i + 1) * HD], sc)
-            sbuf[grp & 1, hp] = jnp.where(valid, sc * (HD ** -0.5), -jnp.inf)
-
-    def soften_group(grp):
-        rows = rows_of(grp)
-        for hp in range(HEADS // 2):
-            sc = sbuf[grp & 1, hp]
-            self_sc = jnp.sum(pair_of(qbuf, rows, hp) * pair_of(nkbuf, rows, hp), axis=-1, keepdims=True) * (HD ** -0.5)
+            sbuf[unit & 1, n] = jnp.where(valid, sc * (HD ** -0.5), -jnp.inf)
+
+    def soften_unit(unit):
+        for n, at, rows, cols in parts_of(unit):
+            sc = sbuf[unit & 1, n]
+            q_k = [jnp.concatenate([ref[rows, c] for c in cols], axis=0) for ref in (qbuf, nkbuf)]
+            self_sc = jnp.sum(q_k[0] * q_k[1], axis=-1, keepdims=True) * (HD ** -0.5)
             peak = jnp.maximum(jnp.max(sc, axis=-1, keepdims=True), self_sc)
             wts = jnp.exp(sc - peak)
             self_w = jnp.exp(self_sc - peak)
@@ -149,45 +165,44 @@
             prob = wts / denom
             self_p = (self_w / denom).astype(BF16).astype(F32)
             wide = jnp.concatenate([jnp.where(row_id == i, prob, 0.0) for i in range(GROUP)], axis=1).astype(BF16)
-            pbuf[grp & 1, hp] = wide
+            pbuf[unit & 1, n] = wide
             for p in range(2):
-                cols = slice((2 * hp + p) * HD, (2 * hp + p + 1) * HD)
-                cbuf[rows, cols] = self_p[p * GROUP:(p + 1) * GROUP] * nvbuf[rows, cols]
-
-    def value_group(grp):
-        slot = grp & (KV_RING - 1)
-        rows = rows_of(grp)
-        for hp in range(HEADS // 2):
-            rhs = jnp.concatenate([vbuf[slot, 2 * hp], vbuf[slot, 2 * hp + 1]], axis=1)
-            ctx = jnp.dot(pbuf[grp & 1, hp], rhs, preferred_element_type=F32)
+                cbuf[rows, cols[p]] = self_p[p * GROUP:(p + 1) * GROUP] * nvbuf[rows, cols[p]]
+
+    def value_unit(unit):
+        slot = unit & (KV_RING - 1)
+        for n, at, rows, cols in parts_of(unit):
+            rhs = jnp.concatenate([vbuf[slot, at], vbuf[slot, at + 1]], axis=1)
+            ctx = jnp.dot(pbuf[unit & 1, n], rhs, preferred_element_type=F32)
             for p in range(2):
-                cols = slice((2 * hp + p) * HD, (2 * hp + p + 1) * HD)
-                cbuf[rows, cols] += ctx[p * GROUP:(p + 1) * GROUP, p * HD:(p + 1) * HD]
-
-    last = groups - 1
-    wait_group(jnp.int32(0), kbuf, ksem)
-    score_group(jnp.int32(0))
-    wait_group(jnp.int32(1), kbuf, ksem)
-    soften_group(jnp.int32(0))
-    score_group(jnp.int32(1))
-
-    def body(grp, carry):
-        wait_group(grp - 1, vbuf, vsem)
-        wait_group(grp + 1, kbuf, ksem)
-        value_group(grp - 1)
-        soften_group(grp)
-        score_group(grp + 1)
-
-        @pl.when(grp - 1 + KV_RING < groups)
+                cbuf[rows, cols[p]] += ctx[p * GROUP:(p + 1) * GROUP, p * HD:(p + 1) * HD]
+
+    last = 2 * PAIRS - 1
+    wait_unit(jnp.int32(0), kbuf, ksem)
+    score_unit(jnp.int32(0))
+    wait_unit(jnp.int32(1), kbuf, ksem)
+    soften_unit(jnp.int32(0))
+    score_unit(jnp.int32(1))
+
+    def body(unit, carry):
+        wait_unit(unit - 1, vbuf, vsem)
+        wait_unit(unit + 1, kbuf, ksem)
+        value_unit(unit - 1)
+        soften_unit(unit)
+        score_unit(unit + 1)
+
+        @pl.when(unit - 1 + KV_RING <= last)
         def _():
-            start_group(grp - 1 + KV_RING)
+            start_unit(unit - 1 + KV_RING)
         return carry
-    lax.fori_loop(1, last, body, 0)
-    wait_group(jnp.int32(last - 1), vbuf, vsem)
-    wait_group(jnp.int32(last), vbuf, vsem)
-    value_group(jnp.int32(last - 1))
-    soften_group(jnp.int32(last))
-    value_group(jnp.int32(last))
+    lax.fori_loop(1, PAIRS - 1, body, 0)
+    project(1)
+    lax.fori_loop(PAIRS - 1, last, body, 0)
+    wait_unit(jnp.int32(last - 1), vbuf, vsem)
+    wait_unit(jnp.int32(last), vbuf, vsem)
+    value_unit(jnp.int32(last - 1))
+    soften_unit(jnp.int32(last))
+    value_unit(jnp.int32(last))
     ctx_ref[...] = cbuf[...].astype(BF16)
 
 
@@ -203,6 +218,9 @@
         out_specs=vmem_spec,
         scratch_shapes=[
             pltpu.VMEM((ROWS, DIM), BF16),
+            pltpu.VMEM((ROWS, DIM), BF16),
+            pltpu.VMEM((ROWS, HD), F32),
+            pltpu.VMEM((ROWS, HD), F32),
             pltpu.VMEM((6, DIM, QW), BF16),
             pltpu.VMEM((ROWS, HD), F32),
             pltpu.VMEM((ROWS, HALF), F32),
@@ -211,12 +229,12 @@
             pltpu.VMEM((ROWS, HALF), F32),
             pltpu.VMEM((2, HEADS // 2, 2 * GROUP, HD), F32),
             pltpu.VMEM((2, HEADS // 2, 2 * GROUP, GROUP * HD), BF16),
-            pltpu.VMEM((KV_RING, HEADS, GROUP * HD, HD), BF16),
-            pltpu.VMEM((KV_RING, HEADS, GROUP * HD, HD), BF16),
+            pltpu.VMEM((KV_RING, 2 * HH, GROUP * HD, HD), BF16),
+            pltpu.VMEM((KV_RING, 2 * HH, GROUP * HD, HD), BF16),
             pltpu.SemaphoreType.DMA,
             pltpu.SemaphoreType.DMA((6,)),
-            pltpu.SemaphoreType.DMA((KV_RING,)),
-            pltpu.SemaphoreType.DMA((KV_RING,)),
+            pltpu.SemaphoreType.DMA((KV_RING, 2)),
+            pltpu.SemaphoreType.DMA((KV_RING, 2)),
         ],
         compiler_params=pltpu.CompilerParams(vmem_limit_bytes=60 * HALF * HALF),
         name='attend',
@@ -311,7 +329,7 @@
         mbuf[core, :, j * QW:(j + 1) * QW] = (xbuf[:, j * QW:(j + 1) * QW].astype(F32) + acc).astype(BF16)
     m_cp = rdma(mbuf.at[core], mbuf.at[core], misc_s.at[S_M], misc_r.at[S_M], sibling)
     m_cp.start()
-    for b in range(9, 18):
+    for b in range(9, 22):
         start_gu_block(b)
     m_other = rdma(mbuf.at[1 - core], mbuf.at[1 - core], misc_s.at[S_M], misc_r.at[S_M], sibling)
     m_other.wait_recv()
@@ -353,8 +371,8 @@
     ish[core] = (jax.nn.silu(gate) * up).astype(BF16)
     ish_cp = rdma(ish.at[core], ish.at[core], misc_s.at[S_IN], misc_r.at[S_IN], sibling)
     ish_cp.start()
-    start_gu_block(18)
-    start_gu_block(19)
+    start_gu_block(22)
+    start_gu_block(23)
 
     expert_id = dy * 32 + cx * EXPERTS + lax.broadcasted_iota(jnp.int32, (EXPERTS, ROWS), 0)
     before = (lax.broadcasted_iota(jnp.int32, (ROWS, ROWS), 0) < lax.broadcasted_iota(jnp.int32, (ROWS, ROWS), 1))
@@ -389,11 +407,14 @@
     for xb in range(2):
         route_block(dy, xb)
 
-    def dispatch(b):
+    half_rows = XE * SLOTS
+
+    def dispatch(b, part):
         def one(n, carry):
             cols = pl.ds(pl.multiple_of(n * QW, QW), QW)
-            rows = jnp.dot(dmat[b], uall[b, :, cols], preferred_element_type=F32).astype(BF16)
-            for e in range(EXPERTS):
+            rows = jnp.dot(dmat[b, part * half_rows:(part + 1) * half_rows, :], uall[b, :, cols],
+                           preferred_element_type=F32).astype(BF16)
+            for e in range(XE):
                 xe[e, pl.ds(pl.multiple_of(b * SLOTS, SLOTS), SLOTS), cols] = rows[e * SLOTS:(e + 1) * SLOTS, :]
             return carry
         lax.fori_loop(0, DIM // QW, one, 0)
@@ -411,8 +432,8 @@
         acc = jnp.dot(ish[0], ring[4, j * HALF:j * HALF + QW, :], preferred_element_type=F32)
         acc = acc + jnp.dot(ish[1], ring[4, j * HALF + QW:(j + 1) * HALF, :], preferred_element_type=F32)
         base[:, j * QW:(j + 1) * QW] = mbuf[core, :, j * QW:(j + 1) * QW].astype(F32) + acc.astype(BF16).astype(F32)
-    start_gu_block(20)
-    dispatch(blk0)
+    start_gu_block(24)
+    dispatch(blk0, 0)
     rdma(ids_all.at[1 - dy], ids_all.at[1 - dy], misc_s.at[S_IDS], misc_r.at[S_IDS], y_nbr).wait_recv()
     rdma(gates_all.at[1 - dy], gates_all.at[1 - dy], misc_s.at[S_GATES], misc_r.at[S_GATES], y_nbr).wait_recv()
     u_copy(blk_x, 1, X_LINK, x_nbr).wait_recv()
@@ -423,17 +444,17 @@
         route_block(1 - dy, xb)
     for h in range(2):
         u_fwd(blk_x, 1 - core, X_LINK, h).wait_recv()
-    dispatch(blk_x)
+    dispatch(blk_x, 0)
     u_copy(blk_d, 0, RELAY, y_nbr).wait_recv()
     u_fwd(blk_d, core, RELAY, 0).start()
     u_copy(blk_d, 1, RELAY, x_nbr).wait_recv()
     u_fwd(blk_d, core, RELAY, 1).start()
     for h in range(2):
         u_fwd(blk_y, 1 - core, Y_LINK, h).wait_recv()
-    dispatch(blk_y)
+    dispatch(blk_y, 0)
     for h in range(2):
         u_fwd(blk_d, 1 - core, RELAY, h).wait_recv()
-    dispatch(blk_d)
+    dispatch(blk_d, 0)
 
     def in_part(e, c):
         return inner.at[e, :, pl.ds(pl.multiple_of(c * QW, QW), QW)]
@@ -442,12 +463,12 @@
         return rdma(in_part(e, c), in_part(e, c), in_s.at[e], in_r.at[e], sibling)
 
     def expert_pair(p, after):
-        slots = [((5 + 4 * p + i) & (RING - 1)) for i in range(4)]
+        slots = [lax.rem(5 + 4 * p + i, RING) for i in range(4)]
         for slot in slots:
             wait_slot(slot)
         for i in range(2):
             e = 2 * p + i
-            rows = xe[e]
+            rows = xe[e & (XE - 1)]
             gate = jnp.dot(rows, ring[slots[2 * i]], preferred_element_type=F32)
             up = jnp.dot(rows, ring[slots[2 * i + 1]], preferred_element_type=F32)
             inner[e, :, pl.ds(pl.multiple_of(core * QW, QW), QW)] = (jax.nn.silu(gate) * up).astype(BF16)
@@ -455,17 +476,21 @@
             in_copy(2 * p + i, core).start()
         after(p, slots)
 
-    def refill_experts(p, slots):
-        for i in range(2):
-            start_gate(2 * p + i + 8, slots[2 * i])
-            start_up(2 * p + i + 8, slots[2 * i + 1])
-
-    def refill_down(p, slots):
-        for i in range(4):
-            start_down(4 * (p - 4) + i, slots[i])
-
-    lax.fori_loop(0, 4, lambda p, c: (expert_pair(p, refill_experts), c)[1], 0)
-    lax.fori_loop(4, 8, lambda p, c: (expert_pair(p, refill_down), c)[1], 0)
+    def refill(p, slots):
+        @pl.when(p < 3)
+        def _():
+            for i in range(2):
+                start_gate(2 * p + i + 10, slots[2 * i])
+                start_up(2 * p + i + 10, slots[2 * i + 1])
+
+        @pl.when((p >= 3) & (p < 7))
+        def _():
+            for i in range(4):
+                start_down(4 * (p - 3) + i, slots[i])
+
+    lax.fori_loop(0, 4, lambda p, c: (expert_pair(p, refill), c)[1], 0)
+    lax.fori_loop(0, 4, lambda b, c: (dispatch(b, 1), c)[1], 0)
+    lax.fori_loop(4, 8, lambda p, c: (expert_pair(p, refill), c)[1], 0)
 
     top = pl.ds(0, ROWS_Y)
     low = pl.ds(ROWS_Y, ROWS - ROWS_Y)
@@ -529,7 +554,7 @@
 
     for k in range(CHUNKS):
         def down_group(g, carry):
-            slot = (5 + 4 * k + g) & (RING - 1)
+            slot = lax.rem(37 + 4 * k + g, RING)
             wait_slot(slot)
             for i in range(4):
                 e = g * 4 + i
@@ -614,7 +639,7 @@
             pltpu.VMEM((2, 8, 2 * ROWS), F32),
             pltpu.VMEM((4, EXPERTS * SLOTS, ROWS), BF16),
             pltpu.VMEM((4, 3 * ROWS, EXPERTS * SLOTS), BF16),
-            pltpu.VMEM((EXPERTS, 4 * SLOTS, DIM), BF16),
+            pltpu.VMEM((XE, 4 * SLOTS, DIM), BF16),
             pltpu.VMEM((EXPERTS, 4 * SLOTS, HALF), BF16),
             pltpu.VMEM((4, EXPERTS * SLOTS, CW), BF16),
             pltpu.VMEM((CHUNKS, 4, ROWS, CW), F32),
@@ -629,7 +654,7 @@
             dma((CHUNKS,)), dma((CHUNKS,)), dma((CHUNKS,)), dma((CHUNKS,)), dma((CHUNKS,)), dma((CHUNKS,)),
             dma((4, CHUNKS)),
         ],
-        compiler_params=pltpu.CompilerParams(vmem_limit_bytes=60 * HALF * HALF, collective_id=0, has_side_effects=True),
+        compiler_params=pltpu.CompilerParams(vmem_limit_bytes=63 * HALF * HALF, collective_id=0, has_side_effects=True),
         name='experts',
     )(gain, ctx, ids, gates, hidden, w_o, sg, su, sd, wg, wu, wd)
 

time: 96.5 us -> 97.5 us (1.010)
    pallas_call x1, Pallas kernels: 25.4 us -> 26.4 us  [attention(): pl.pallas_call(attn_kernel, out_shape=jax.ShapeDtypeStruct((ROWS, HALF),...]
where the time goes in v3:
time: 97.5 us; the launch traced here: 97.1 us
  Pallas kernels  94.8 us (97%)
  local copies, waits for them, and re-layouts  2.3 us (2%)
    pallas_call x1, Pallas kernels, moe(): pl.pallas_call(moe_kernel, out_shape=jax.ShapeDtypeStruct(hidden.shape, B...  68.4 us
    pallas_call x1, Pallas kernels, attention(): pl.pallas_call(attn_kernel, out_shape=jax.ShapeDtypeStruct((ROWS, HALF),...  26.4 us
    unnamed x1, local copies, waits for them, and re-layouts  2.3 us

profile of v3, /device:TPU:0, one launch (start us, length us, event | category | flops | bytes accessed | tf_op | source)
XLA Modules:
  0.0 97.1 jit_solution(9172845868401159520)
XLA Ops:
  0.0 26.4 %attend.1.ctx_ref = bf16[128,1024]{1,0:T(8,128)(2,1)} custom-call(s32[256]{0:T(256)} %lens_ref.1, bf16[256,2048]{1,0:T(8,128)(2,1)} %hidden_ref.3, f32[1,2048]{1,0:T(1,128)} %gain_ref.2, f32[1,128]{1,0:T(1,128)} %constant.2.clone.freq_ref, bf16[1,2048,2048]{2,1,0:T(8,128)(2,1)} %wq_ref.1, bf16[1,2048,4096]{2,1,0:T(8,128)(2,1)} %wkv_ref.1, ...), custom_call_target="tpu_custom_call" | custom-call | tf_op jit(solution)/shard_map/attend/pallas_call | solution.py:214
  26.4 68.4 %experts.1 = bf16[256,2048]{1,0:T(8,128)(2,1)} custom-call(f32[1,2048]{1,0:T(1,128)} %gain_ref.3, bf16[128,1024]{1,0:T(8,128)(2,1)} %attend.1.ctx_ref, s32[8,256]{1,0:T(8,128)} %bitcast.6, f32[8,256]{1,0:T(8,128)} %bitcast.7, bf16[256,2048]{1,0:T(8,128)(2,1)} %hidden_ref.3, bf16[1,2048,2048]{2,1,0:T(8,128)(2,1)} %wo_ref.1, bf16[1,2048,1024]{2,1,0:T(8,128)(2,1)} %sg_ref.1, ...), custom_call_target="tpu_custom_call" | custom-call | tf_op jit(solution)/shard_map/experts/pallas_call | solution.py:624
  94.8 2.3 %copy.20 = bf16[256,2048]{1,0:T(8,128)(2,1)} copy(bf16[256,2048]{1,0:T(8,128)(2,1)} %experts.1) | data formatting | bytes 2097152

commit v4 on v3

--- a/solution.py
+++ b/solution.py
@@ -34,7 +34,7 @@
 SLOTS = 32
 CHUNKS = 4
 CW = HALF // CHUNKS
-ROWS_Y = 96
+ROWS_Y = (72, 104, 72, 64)
 
 
 def norm_rows(rows_f, gain):
@@ -49,11 +49,8 @@
     core = side % 2
     h0 = core * HEADS
 
-    def size_of(unit, tok):
+    def size_of(tok):
         return (lens_ref[row0 + tok] + 15) & -16
-
-    def v_size_of(unit, tok):
-        return jnp.where(unit < KV_RING, HD, size_of(unit, tok))
 
     def first_token(unit, d):
         return (unit & (PAIRS - 1)) * (2 * GROUP) + d * GROUP
@@ -64,16 +61,15 @@
         for d in range(2):
             for i in range(GROUP):
                 tok = first_token(unit, d) + i
-                for src, dst, sem, size in ((kc_ref, kbuf, ksem, size_of), (vc_ref, vbuf, vsem, v_size_of)):
-                    size = pl.multiple_of(size(unit, tok), 16)
+                size = pl.multiple_of(size_of(tok), 16)
+                for src, dst, sem in ((kc_ref, kbuf, ksem), (vc_ref, vbuf, vsem)):
                     pltpu.make_async_copy(src.at[LAYER, row0 + tok, heads, pl.ds(0, size), :],
                                           dst.at[slot, pl.ds(d * HH, HH), pl.ds(i * HD, size), :], sem.at[slot, d]).start()
 
     def wait_unit(unit, buf, sem):
         slot = unit & (KV_RING - 1)
-        size = size_of if buf is kbuf else v_size_of
         for d in range(2):
-            total = sum(size(unit, first_token(unit, d) + i) for i in range(GROUP))
+            total = sum(size_of(first_token(unit, d) + i) for i in range(GROUP))
             whole = buf.at[slot, pl.ds(d * HH, HH), pl.ds(0, pl.multiple_of(total, 16)), :]
             pltpu.make_async_copy(whole, whole, sem.at[slot, d]).wait()
 
@@ -89,7 +85,12 @@
         return pltpu.make_async_copy(src, wbuf.at[j * 3 + kind], wsem.at[j * 3 + kind])
 
     def start_units(lo, hi):
-        lax.fori_loop(lo, hi, lambda u, c: (start_unit(u), c)[1], 0)
+        def one(unit, carry):
+            for h in range(2 * HH):
+                vbuf[unit, h] = jnp.zeros((GROUP * HD, HD), BF16)
+            start_unit(unit)
+            return carry
+        lax.fori_loop(lo, hi, one, 0)
     for kind in range(3):
         weight_copy(0, kind).start()
 
@@ -492,10 +493,11 @@
     lax.fori_loop(0, 4, lambda b, c: (dispatch(b, 1), c)[1], 0)
     lax.fori_loop(4, 8, lambda p, c: (expert_pair(p, refill), c)[1], 0)
 
-    top = pl.ds(0, ROWS_Y)
-    low = pl.ds(ROWS_Y, ROWS - ROWS_Y)
+    def split(k):
+        return pl.ds(0, ROWS_Y[k]), pl.ds(ROWS_Y[k], ROWS - ROWS_Y[k])
 
     def stage1(k, i):
+        top, low = split(k)
         if i == 0:
             return [rdma(pbuf.at[k, blk_d, part, :], recv1.at[k, 0, part, :], p1_s.at[k, 0, a], p1_r.at[k, 0, a], dev)
                     for a, (part, dev) in enumerate(((top, y_nbr), (low, x_nbr)))]
@@ -504,34 +506,36 @@
 
     def stage2(k):
         return [rdma(send2.at[k, part, :], recv2.at[k, part, :], p2_s.at[k, a], p2_r.at[k, a], dev)
-                for a, (part, dev) in enumerate(((top, x_nbr), (low, y_nbr)))]
+                for a, (part, dev) in enumerate(zip(split(k), (x_nbr, y_nbr)))]
 
     def run_stage2(k):
         first, second = stage1(k, 0)
         going = stage2(k)
         first.wait_recv()
-        send2[k, 0:ROWS_Y, :] = pbuf[k, blk_x, 0:ROWS_Y, :] + recv1[k, 0, 0:ROWS_Y, :]
+        n = ROWS_Y[k]
+        send2[k, 0:n, :] = pbuf[k, blk_x, 0:n, :] + recv1[k, 0, 0:n, :]
         going[0].start()
         second.wait_recv()
-        send2[k, ROWS_Y:ROWS, :] = pbuf[k, blk_y, ROWS_Y:ROWS, :] + recv1[k, 0, ROWS_Y:ROWS, :]
+        send2[k, n:ROWS, :] = pbuf[k, blk_y, n:ROWS, :] + recv1[k, 0, n:ROWS, :]
         going[1].start()
 
     def o_part(x, c, k):
         return oall.at[x, c, k]
 
     def store_out(x, c, k, which):
-        return pltpu.make_async_copy(o_part(x, c, k),
-                                     out_ref.at[pl.ds(x * ROWS, ROWS), pl.ds(pl.multiple_of(c * HALF + k * CW, CW), CW)],
-                                     out_sem.at[which, k])
+        return pltpu.make_async_copy(o_part(x, c, k), out_part(x, c, k), out_sem.at[which, k])
+
+    def out_part(x, c, k):
+        return out_ref.at[pl.ds(x * ROWS, ROWS), pl.ds(pl.multiple_of(c * HALF + k * CW, CW), CW)]
 
     def o_sib(k, c):
-        return rdma(o_part(cx, c, k), o_part(cx, c, k), os_s.at[k], os_r.at[k], sibling)
+        return rdma(o_part(cx, c, k), out_part(cx, c, k), os_s.at[k], os_r.at[k], sibling)
 
     def o_x(k, x):
         return rdma(o_part(x, core, k), o_part(x, core, k), ox_s.at[k], ox_r.at[k], x_nbr)
 
     def o_fwd(k, c):
-        return rdma(o_part(1 - cx, c, k), o_part(1 - cx, c, k), of_s.at[k], of_r.at[k], sibling)
+        return rdma(o_part(1 - cx, c, k), out_part(1 - cx, c, k), of_s.at[k], of_r.at[k], sibling)
 
     def run_final(k):
         for cp in stage1(k, 1):
@@ -549,13 +553,13 @@
         o_fwd(k, core).start()
         store_out(1 - cx, core, k, 1).start()
 
-    for e in range(EXPERTS):
-        in_copy(e, 1 - core).wait_recv()
-
     for k in range(CHUNKS):
         def down_group(g, carry):
             slot = lax.rem(37 + 4 * k + g, RING)
             wait_slot(slot)
+            if k == 0:
+                for i in range(4):
+                    in_copy(g * 4 + i, 1 - core).wait_recv()
             for i in range(4):
                 e = g * 4 + i
                 w = ring[slot, (i // 2) * HALF:(i // 2 + 1) * HALF, (i % 2) * CW:(i % 2 + 1) * CW]
@@ -578,20 +582,16 @@
         combine(blk0)
         if k >= 1:
             run_stage2(k - 1)
-        if k >= 2:
-            run_final(k - 2)
+    run_final(0)
     run_stage2(CHUNKS - 1)
-    run_final(CHUNKS - 2)
-    for k in range(CHUNKS - 1):
-        run_forward(k)
-    run_final(CHUNKS - 1)
+    for k in range(1, CHUNKS):
+        run_final(k)
+        run_forward(k - 1)
     run_forward(CHUNKS - 1)
     for k in range(CHUNKS):
         o_sib(k, 1 - core).wait_recv()
-        store_out(cx, 1 - core, k, 2).start()
     for k in range(CHUNKS):
         o_fwd(k, 1 - core).wait_recv()
-        store_out(1 - cx, 1 - core, k, 3).start()
 
     for cp in (ctx_cp, m_cp, ids_cp, gates_cp, ish_cp):
         cp.wait_send()
@@ -613,8 +613,6 @@
         o_fwd(k, core).wait_send()
         store_out(cx, core, k, 0).wait()
         store_out(1 - cx, core, k, 1).wait()
-        store_out(cx, 1 - core, k, 2).wait()
-        store_out(1 - cx, 1 - core, k, 3).wait()
 
 
 def moe(ctx, ids, gates, gain, hidden, w_o, sg, su, sd, wg, wu, wd):
@@ -652,7 +650,7 @@
             dma((EXPERTS,)), dma((EXPERTS,)),
             dma((CHUNKS, 2, 2)), dma((CHUNKS, 2, 2)), dma((CHUNKS, 2)), dma((CHUNKS, 2)),
             dma((CHUNKS,)), dma((CHUNKS,)), dma((CHUNKS,)), dma((CHUNKS,)), dma((CHUNKS,)), dma((CHUNKS,)),
-            dma((4, CHUNKS)),
+            dma((2, CHUNKS)),
         ],
         compiler_params=pltpu.CompilerParams(vmem_limit_bytes=63 * HALF * HALF, collective_id=0, has_side_effects=True),
         name='experts',

time: 97.5 us -> 93.1 us (0.955)
  Pallas kernels: 94.8 us -> 90.6 us
    pallas_call x1, Pallas kernels: 68.4 us -> 64.7 us  [moe(): pl.pallas_call(moe_kernel, out_shape=jax.ShapeDtypeStruct(hidden.shape, B...]
where the time goes in v4:
time: 93.1 us; the launch traced here: 92.9 us
  Pallas kernels  90.6 us (97%)
  local copies, waits for them, and re-layouts  2.3 us (2%)
    pallas_call x1, Pallas kernels, moe(): pl.pallas_call(moe_kernel, out_shape=jax.ShapeDtypeStruct(hidden.shape, B...  64.7 us
    pallas_call x1, Pallas kernels, attention(): pl.pallas_call(attn_kernel, out_shape=jax.ShapeDtypeStruct((ROWS, HALF),...  25.8 us
    unnamed x1, local copies, waits for them, and re-layouts  2.3 us

profile of v4, /device:TPU:0, one launch (start us, length us, event | category | flops | bytes accessed | tf_op | source)
XLA Modules:
  0.0 92.9 jit_solution(10623666083079095602)
XLA Ops:
  0.0 25.8 %attend.1.ctx_ref = bf16[128,1024]{1,0:T(8,128)(2,1)} custom-call(s32[256]{0:T(256)} %lens_ref.1, bf16[256,2048]{1,0:T(8,128)(2,1)} %hidden_ref.3, f32[1,2048]{1,0:T(1,128)} %gain_ref.2, f32[1,128]{1,0:T(1,128)} %constant.2.clone.freq_ref, bf16[1,2048,2048]{2,1,0:T(8,128)(2,1)} %wq_ref.1, bf16[1,2048,4096]{2,1,0:T(8,128)(2,1)} %wkv_ref.1, ...), custom_call_target="tpu_custom_call" | custom-call | tf_op jit(solution)/shard_map/attend/pallas_call | solution.py:215
  25.8 64.7 %experts.1 = bf16[256,2048]{1,0:T(8,128)(2,1)} custom-call(f32[1,2048]{1,0:T(1,128)} %gain_ref.3, bf16[128,1024]{1,0:T(8,128)(2,1)} %attend.1.ctx_ref, s32[8,256]{1,0:T(8,128)} %bitcast.6, f32[8,256]{1,0:T(8,128)} %bitcast.7, bf16[256,2048]{1,0:T(8,128)(2,1)} %hidden_ref.3, bf16[1,2048,2048]{2,1,0:T(8,128)(2,1)} %wo_ref.1, bf16[1,2048,1024]{2,1,0:T(8,128)(2,1)} %sg_ref.1, ...), custom_call_target="tpu_custom_call" | custom-call | tf_op jit(solution)/shard_map/experts/pallas_call | solution.py:622
  90.6 2.3 %copy.20 = bf16[256,2048]{1,0:T(8,128)(2,1)} copy(bf16[256,2048]{1,0:T(8,128)(2,1)} %experts.1) | data formatting | bytes 2097152

commit v5 on v4

--- a/solution.py
+++ b/solution.py
@@ -27,7 +27,8 @@
 RING = 20
 QW = 512
 LAYER = 0
-S_CTX, S_IDS, S_M, S_IN, S_GATES = range(5)
+S_PART, S_IDS, S_M, S_IN, S_GATES, S_U = range(6)
+CORE_ROWS = ROWS // 2
 X_LINK, Y_LINK, RELAY = range(3)
 XE = 8
 EXPERTS = 16
@@ -42,8 +43,8 @@
     return (rows_f * inv_rms * gain).astype(BF16)
 
 
-def attn_kernel(lens_ref, hidden_ref, gain_ref, freq_ref, wq_ref, wkv_ref, kc_ref, vc_ref, ctx_ref,
-                xbuf, nbuf, cosbuf, sinbuf, wbuf, pos_buf, qbuf, nkbuf, nvbuf, cbuf, sbuf, pbuf, kbuf, vbuf, xsem, wsem, ksem, vsem):
+def attn_kernel(lens_hbm, hidden_ref, gain_hbm, freq_hbm, wq_ref, wkv_ref, kc_ref, vc_ref, ctx_ref,
+                lens_ref, gain_ref, freq_ref, small_sem, xbuf, nbuf, cosbuf, sinbuf, wbuf, pos_buf, qbuf, nkbuf, nvbuf, cbuf, sbuf, pbuf, kbuf, vbuf, xsem, wsem, ksem, vsem):
     side = lax.axis_index('side')
     row0 = (side // 2) * ROWS
     core = side % 2
@@ -73,6 +74,10 @@
             whole = buf.at[slot, pl.ds(d * HH, HH), pl.ds(0, pl.multiple_of(total, 16)), :]
             pltpu.make_async_copy(whole, whole, sem.at[slot, d]).wait()
 
+    small = [pltpu.make_async_copy(src, dst, small_sem.at[i])
+             for i, (src, dst) in enumerate(((lens_hbm, lens_ref), (freq_hbm, freq_ref), (gain_hbm, gain_ref)))]
+    for cp in small:
+        cp.start()
     x_cp = pltpu.make_async_copy(hidden_ref.at[pl.ds(row0, ROWS), :], xbuf, xsem)
     x_cp.start()
 
@@ -93,6 +98,9 @@
         lax.fori_loop(lo, hi, one, 0)
     for kind in range(3):
         weight_copy(0, kind).start()
+
+    for cp in small:
+        cp.wait()
 
     def fill_pos(i, carry):
         for r in range(8):
@@ -215,9 +223,13 @@
     return pl.pallas_call(
         attn_kernel,
         out_shape=jax.ShapeDtypeStruct((ROWS, HALF), BF16),
-        in_specs=[pl.BlockSpec(memory_space=pltpu.SMEM), any_spec, vmem_spec, vmem_spec] + [any_spec] * 4,
+        in_specs=[any_spec] * 8,
         out_specs=vmem_spec,
         scratch_shapes=[
+            pltpu.SMEM(lens.shape, jnp.int32),
+            pltpu.VMEM((1, DIM), F32),
+            pltpu.VMEM((1, HD), F32),
+            pltpu.SemaphoreType.DMA((3,)),
             pltpu.VMEM((ROWS, DIM), BF16),
             pltpu.VMEM((ROWS, DIM), BF16),
             pltpu.VMEM((ROWS, HD), F32),
@@ -242,8 +254,8 @@
     )(lens, hidden, gain, jnp.asarray(freq), w_q, w_kv, k_cache, v_cache)
 
 
-def moe_kernel(gain_ref, ctx_ref, ids_ref, gates_ref, hidden_ref, wo_ref, sg_ref, su_ref, sd_ref, wg_ref, wu_ref, wd_ref, out_ref,
-               ring, ctx_own, ctx_sib, xbuf, mbuf, uall, ish, base, ids_all, gates_all, dmat, cg, xe, inner, ybuf, pbuf,
+def moe_kernel(gain_hbm, ctx_ref, ids_ref, gates_ref, hidden_ref, wo_ref, sg_ref, su_ref, sd_ref, wg_ref, wu_ref, wd_ref, out_ref,
+               gain_ref, ring, ctx_own, part, part_in, xbuf, mrow, mhalf, uall, ish, base, ids_all, gates_all, dmat, cg, xe, inner, ybuf, pbuf,
                recv1, send2, recv2, oall,
                ring_sem, x_sem, misc_s, misc_r, u_s, u_r, uf_s, uf_r, in_s, in_r, p1_s, p1_r, p2_s, p2_r,
                os_s, os_r, ox_s, ox_r, of_s, of_r, out_sem):
@@ -266,7 +278,9 @@
                                             device_id=dev, device_id_type=MESH)
 
     def start_wo(j):
-        pltpu.make_async_copy(wo_ref.at[LAYER, :, pl.ds(col0 + j * QW, QW)], ring.at[j], ring_sem.at[j]).start()
+        for q in range(2):
+            pltpu.make_async_copy(wo_ref.at[LAYER, pl.ds(col0, HALF), pl.ds((2 * j + q) * QW, QW)],
+                                  ring.at[j, pl.ds(q * HALF, HALF), :], ring_sem.at[j]).start()
 
     def start_gate(e, slot):
         pltpu.make_async_copy(wg_ref.at[LAYER, cx * EXPERTS + e, :, pl.ds(core * QW, QW)], ring.at[slot], ring_sem.at[slot]).start()
@@ -293,8 +307,12 @@
     ctx_in.start()
     start_wo(0)
     start_wo(1)
-    x_cp = pltpu.make_async_copy(hidden_ref.at[pl.ds(cx * ROWS, ROWS), pl.ds(col0, HALF)], xbuf, x_sem.at[1])
+    own_rows = pl.ds(pl.multiple_of(core * CORE_ROWS, CORE_ROWS), CORE_ROWS)
+    sib_rows = pl.ds(pl.multiple_of((1 - core) * CORE_ROWS, CORE_ROWS), CORE_ROWS)
+    x_cp = pltpu.make_async_copy(hidden_ref.at[pl.ds(cx * ROWS + core * CORE_ROWS, CORE_ROWS), :], xbuf, x_sem.at[1])
     x_cp.start()
+    gain_cp = pltpu.make_async_copy(gain_hbm, gain_ref, x_sem.at[4])
+    gain_cp.start()
 
     barrier = pltpu.get_barrier_semaphore()
     for dev in (sibling, x_nbr, y_nbr):
@@ -308,38 +326,25 @@
     pl.semaphore_wait(barrier, 3)
 
     ctx_in.wait()
-    ctx_cp = rdma(ctx_own, ctx_sib, misc_s.at[S_CTX], misc_r.at[S_CTX], sibling)
-    ctx_cp.start()
-
-    own_row = core * HALF
-    sib_row = (1 - core) * HALF
-    wait_slot(0)
-    wait_slot(1)
+    ctx_val = ctx_own[...]
+    for j in range(2):
+        wait_slot(j)
+        for q in range(2):
+            n = 2 * j + q
+            part[:, n * QW:(n + 1) * QW] = jnp.dot(ctx_val, ring[j, q * HALF:(q + 1) * HALF, :], preferred_element_type=F32)
+    part_cp = rdma(part.at[sib_rows, :], part_in, misc_s.at[S_PART], misc_r.at[S_PART], sibling)
+    part_cp.start()
     for j in range(2):
         pltpu.make_async_copy(sd_ref.at[LAYER, :, pl.ds(col0 + j * QW, QW)], ring.at[4, pl.ds(j * HALF, HALF), :],
                               ring_sem.at[4]).start()
     for b in range(5, 9):
         start_gu_block(b)
     x_cp.wait()
-    ctx_val = ctx_own[...]
-    accs = [jnp.dot(ctx_val, ring[j, pl.ds(own_row, HALF), :], preferred_element_type=F32) for j in range(2)]
-    ctx_cp.wait_recv()
-    ctx_val = ctx_sib[...]
-    for j in range(2):
-        acc = accs[j] + jnp.dot(ctx_val, ring[j, pl.ds(sib_row, HALF), :], preferred_element_type=F32)
-        mbuf[core, :, j * QW:(j + 1) * QW] = (xbuf[:, j * QW:(j + 1) * QW].astype(F32) + acc).astype(BF16)
-    m_cp = rdma(mbuf.at[core], mbuf.at[core], misc_s.at[S_M], misc_r.at[S_M], sibling)
-    m_cp.start()
-    for b in range(9, 22):
-        start_gu_block(b)
-    m_other = rdma(mbuf.at[1 - core], mbuf.at[1 - core], misc_s.at[S_M], misc_r.at[S_M], sibling)
-    m_other.wait_recv()
-    m_lo = mbuf[0].astype(F32)
-    m_hi = mbuf[1].astype(F32)
-    total = jnp.sum(m_lo * m_lo, axis=-1, keepdims=True) + jnp.sum(m_hi * m_hi, axis=-1, keepdims=True)
-    inv_rms = lax.rsqrt(total / DIM + NORM_EPS)
-    uall[blk0, :, 0:HALF] = (m_lo * inv_rms * gain_ref[:, 0:HALF]).astype(BF16)
-    uall[blk0, :, HALF:DIM] = (m_hi * inv_rms * gain_ref[:, HALF:DIM]).astype(BF16)
+    gain_cp.wait()
+    part_cp.wait_recv()
+    mid_rows = (xbuf[...].astype(F32) + (part[own_rows, :] + part_in[...])).astype(BF16)
+    mrow[...] = mid_rows
+    uall[blk0, own_rows, :] = norm_rows(mid_rows.astype(F32), gain_ref[...])
 
     blk_x = dy * 2 + 1 - cx
     blk_y = (1 - dy) * 2 + cx
@@ -357,6 +362,16 @@
     u_copy(blk0, 1, Y_LINK, y_nbr).start()
     u_copy(blk0, 1, X_LINK, x_nbr).start()
     u_copy(blk0, 0, Y_LINK, y_nbr).start()
+    own_cols = pl.ds(pl.multiple_of(col0, HALF), HALF)
+    sib_cols = pl.ds(pl.multiple_of((1 - core) * HALF, HALF), HALF)
+    u_sib = [rdma(uall.at[blk0, rows, :], uall.at[blk0, rows, :], misc_s.at[S_U], misc_r.at[S_U], sibling)
+             for rows in (own_rows, sib_rows)]
+    u_sib[0].start()
+    m_cp = rdma(mrow.at[:, sib_cols], mhalf.at[own_rows, :], misc_s.at[S_M], misc_r.at[S_M], sibling)
+    m_cp.start()
+    mhalf[own_rows, :] = mrow[:, own_cols]
+    for b in range(9, 22):
+        start_gu_block(b)
     ids_in.wait()
     gates_in.wait()
     ids_cp = rdma(ids_all.at[dy], ids_all.at[dy], misc_s.at[S_IDS], misc_r.at[S_IDS], y_nbr)
@@ -366,6 +381,7 @@
 
     wait_slot(2)
     wait_slot(3)
+    u_sib[1].wait_recv()
     u_own = uall[blk0]
     gate = jnp.dot(u_own, ring[2], preferred_element_type=F32)
     up = jnp.dot(u_own, ring[3], preferred_element_type=F32)
@@ -427,12 +443,13 @@
     u_copy(blk_y, 1, RELAY, x_nbr).start()
     u_fwd(blk_y, core, Y_LINK, 1).start()
 
+    rdma(mrow.at[:, sib_cols], mhalf.at[sib_rows, :], misc_s.at[S_M], misc_r.at[S_M], sibling).wait_recv()
     rdma(ish.at[1 - core], ish.at[1 - core], misc_s.at[S_IN], misc_r.at[S_IN], sibling).wait_recv()
     wait_slot(4)
     for j in range(2):
         acc = jnp.dot(ish[0], ring[4, j * HALF:j * HALF + QW, :], preferred_element_type=F32)
         acc = acc + jnp.dot(ish[1], ring[4, j * HALF + QW:(j + 1) * HALF, :], preferred_element_type=F32)
-        base[:, j * QW:(j + 1) * QW] = mbuf[core, :, j * QW:(j + 1) * QW].astype(F32) + acc.astype(BF16).astype(F32)
+        base[:, j * QW:(j + 1) * QW] = mhalf[:, j * QW:(j + 1) * QW].astype(F32) + acc.astype(BF16).astype(F32)
     start_gu_block(24)
     dispatch(blk0, 0)
     rdma(ids_all.at[1 - dy], ids_all.at[1 - dy], misc_s.at[S_IDS], misc_r.at[S_IDS], y_nbr).wait_recv()
@@ -593,7 +610,7 @@
     for k in range(CHUNKS):
         o_fwd(k, 1 - core).wait_recv()
 
-    for cp in (ctx_cp, m_cp, ids_cp, gates_cp, ish_cp):
+    for cp in (part_cp, m_cp, u_sib[0], ids_cp, gates_cp, ish_cp):
         cp.wait_send()
     for h in range(2):
         u_copy(blk0, h, X_LINK, x_nbr).wait_send()
@@ -617,19 +634,21 @@
 
 def moe(ctx, ids, gates, gain, hidden, w_o, sg, su, sd, wg, wu, wd):
     any_spec = pl.BlockSpec(memory_space=pl.ANY)
-    vmem_spec = pl.BlockSpec(memory_space=pltpu.VMEM)
     dma = pltpu.SemaphoreType.DMA
     return pl.pallas_call(
         moe_kernel,
         out_shape=jax.ShapeDtypeStruct(hidden.shape, BF16),
-        in_specs=[vmem_spec] + [any_spec] * 11,
+        in_specs=[any_spec] * 12,
         out_specs=any_spec,
         scratch_shapes=[
+            pltpu.VMEM((1, DIM), F32),
             pltpu.VMEM((RING, DIM, QW), BF16),
             pltpu.VMEM((ROWS, HALF), BF16),
+            pltpu.VMEM((ROWS, DIM), F32),
+            pltpu.VMEM((CORE_ROWS, DIM), F32),
+            pltpu.VMEM((CORE_ROWS, DIM), BF16),
+            pltpu.VMEM((CORE_ROWS, DIM), BF16),
             pltpu.VMEM((ROWS, HALF), BF16),
-            pltpu.VMEM((ROWS, HALF), BF16),
-            pltpu.VMEM((2, ROWS, HALF), BF16),
             pltpu.VMEM((4, ROWS, DIM), BF16),
             pltpu.VMEM((2, ROWS, QW), BF16),
             pltpu.VMEM((ROWS, HALF), F32),
@@ -645,7 +664,7 @@
             pltpu.VMEM((CHUNKS, ROWS, CW), F32),
             pltpu.VMEM((CHUNKS, ROWS, CW), F32),
             pltpu.VMEM((2, 2, CHUNKS, ROWS, CW), BF16),
-            dma((RING,)), dma((4,)), dma((5,)), dma((5,)),
+            dma((RING,)), dma((5,)), dma((6,)), dma((6,)),
             dma((3, 2)), dma((3, 2)), dma((3, 2)), dma((3, 2)),
             dma((EXPERTS,)), dma((EXPERTS,)),
             dma((CHUNKS, 2, 2)), dma((CHUNKS, 2, 2)), dma((CHUNKS, 2)), dma((CHUNKS, 2)),

time: 93.1 us -> 91.7 us (0.985)
  Pallas kernels: 90.6 us -> 89.3 us
where the time goes in v5:
time: 91.7 us; the launch traced here: 91.6 us
  Pallas kernels  89.3 us (97%)
  local copies, waits for them, and re-layouts  2.3 us (3%)
    pallas_call x1, Pallas kernels, moe(): pl.pallas_call(moe_kernel, out_shape=jax.ShapeDtypeStruct(hidden.shape, B...  64.1 us
    pallas_call x1, Pallas kernels, attention(): pl.pallas_call(attn_kernel, out_shape=jax.ShapeDtypeStruct((ROWS, HALF),...  25.2 us
    unnamed x1, local copies, waits for them, and re-layouts  2.3 us

profile of v5, /device:TPU:0, one launch (start us, length us, event | category | flops | bytes accessed | tf_op | source)
XLA Modules:
  0.0 91.6 jit_solution(8425272328439011042)
XLA Ops:
  0.0 25.2 %attend.1.ctx_ref = bf16[128,1024]{1,0:T(8,128)(2,1)} custom-call(s32[256]{0:T(256)} %lens_hbm.1, bf16[256,2048]{1,0:T(8,128)(2,1)} %hidden_ref.3, f32[1,2048]{1,0:T(1,128)} %gain_hbm.2, f32[1,128]{1,0:T(1,128)} %constant.2.clone.freq_hbm, bf16[1,2048,2048]{2,1,0:T(8,128)(2,1)} %wq_ref.1, bf16[1,2048,4096]{2,1,0:T(8,128)(2,1)} %wkv_ref.1, ...), custom_call_target="tpu_custom_call" | custom-call | tf_op jit(solution)/shard_map/attend/pallas_call | solution.py:223
  25.2 64.1 %experts.1 = bf16[256,2048]{1,0:T(8,128)(2,1)} custom-call(f32[1,2048]{1,0:T(1,128)} %gain_hbm.3, bf16[128,1024]{1,0:T(8,128)(2,1)} %attend.1.ctx_ref, s32[8,256]{1,0:T(8,128)} %bitcast.6, f32[8,256]{1,0:T(8,128)} %bitcast.7, bf16[256,2048]{1,0:T(8,128)(2,1)} %hidden_ref.3, bf16[1,2048,2048]{2,1,0:T(8,128)(2,1)} %wo_ref.1, bf16[1,2048,1024]{2,1,0:T(8,128)(2,1)} %sg_ref.1, ...), custom_call_target="tpu_custom_call" | custom-call | tf_op jit(solution)/shard_map/experts/pallas_call | solution.py:638
  89.3 2.3 %copy.20 = bf16[256,2048]{1,0:T(8,128)(2,1)} copy(bf16[256,2048]{1,0:T(8,128)(2,1)} %experts.1) | data formatting | bytes 2097152
